TPU v7x, 128 devices: a whole 4x4x4 slice. The times are simulated.
128 devices in a mesh: px: 8 (over z_lo, y), py: 16 (over x, z_hi, core).
Axes of the slice: x: 4, y: 4, z: 4 (z_hi: 2, z_lo: 2; z = z_hi * 2 + z_lo), core: 2. Of those that a mesh axis runs over, the one named last changes fastest.
Arguments:
- field: bfloat16 [32, 128, 128, 128], P(None, 'px', 'py'), may hold values from -6 to 6
- spec_fine: bfloat16 [2, 32, 32, 32, 32, 32], P(None, None, None, None, 'px', 'py'), may hold values from -18 to 18
- mix_fine: bfloat16 [32, 32], replicated, may hold values from -1 to 1
- bias_fine: float32 [32], replicated, may hold values from -3 to 3
- spec_coarse: bfloat16 [2, 32, 32, 32, 32, 32], P(None, None, None, None, 'px', 'py'), may hold values from -12 to 12
- mix_coarse: bfloat16 [32, 32], replicated, may hold values from -1 to 1
- bias_coarse: float32 [32], replicated, may hold values from -3 to 3
Outputs:
- output: bfloat16 [32, 128, 128, 128], P(None, 'px', 'py')
All inputs are finite; a program needn't handle non-finite values.
Results may differ from a plain program's by a relative error of at most 0.0085.
Values may be sent and summed in bfloat16 or wider, within the bound.
No kernel may reach another device: no remote copies, remote signals or barrier semaphores. Data moves between devices by JAX's collectives and lax.ppermute only.
A program may use at most 128 MiB of HBM per device.

v0:
```python
import math

import jax
import jax.numpy as jnp
from jax import lax
from jax.sharding import PartitionSpec as P

KX = 32
KY = 32
KZ = 32


highest = lax.Precision.HIGHEST


def phases(cells, modes, offset):
    places = jnp.arange(cells, dtype=jnp.int32)
    frequency = jnp.arange(modes, dtype=jnp.int32) - offset
    windings = places[:, None] * frequency[None, :] % cells
    return windings.astype(jnp.float32) * (2.0 * math.pi / cells)


def forward_table(cells, modes, offset):
    angle = phases(cells, modes, offset)
    return jnp.stack([jnp.cos(angle), -jnp.sin(angle)]).astype(jnp.bfloat16)


def inverse_table(cells, modes, offset):
    angle = phases(cells, modes, offset)
    return jnp.transpose(jnp.stack([jnp.cos(angle), jnp.sin(angle)]), (0, 2, 1))


def depth_inverse(cells, modes):
    angle = phases(cells, modes, 0)
    factor = jnp.where(jnp.arange(modes) == 0, 1.0, 2.0).astype(jnp.float32) / float(
        cells * cells * cells
    )
    return jnp.transpose(
        jnp.stack([factor[None, :] * jnp.cos(angle), -factor[None, :] * jnp.sin(angle)]), (0, 2, 1)
    )


def complex_dot(data, table, form):
    real = jnp.einsum(form, data[0], table[0], precision=highest) - jnp.einsum(
        form, data[1], table[1], precision=highest
    )
    imag = jnp.einsum(form, data[0], table[1], precision=highest) + jnp.einsum(
        form, data[1], table[0], precision=highest
    )
    return jnp.stack([real, imag])


def mix_modes(modes, spectral):
    weights = spectral.astype(jnp.float32)
    form = "ijmk,iojmk->ojmk"
    real = jnp.einsum(form, modes[0], weights[0], precision=highest) - jnp.einsum(
        form, modes[1], weights[1], precision=highest
    )
    imag = jnp.einsum(form, modes[0], weights[1], precision=highest) + jnp.einsum(
        form, modes[1], weights[0], precision=highest
    )
    return jnp.stack([real, imag])


def to_modes(field):
    cells = field.shape[3]
    depth_table = forward_table(cells, KZ, 0)
    column_table = forward_table(cells, KY, KY // 2)
    row_table = forward_table(cells, KX, KX // 2).astype(jnp.float32)
    depth = jnp.einsum("cxyz,rzk->rcxyk", field, depth_table, preferred_element_type=jnp.float32)
    depth = lax.all_to_all(depth, "py", split_axis=4, concat_axis=3, tiled=True)
    across = complex_dot(depth, column_table.astype(jnp.float32), "cxyk,ym->cxmk")
    across = lax.all_to_all(across, "px", split_axis=3, concat_axis=2, tiled=True)
    modes = complex_dot(across, row_table, "cxmk,xj->cjmk")
    return modes


def from_modes(mixed, cells):
    row_inverse = inverse_table(cells, KX, KX // 2)
    column_inverse = inverse_table(cells, KY, KY // 2)
    depth_back = depth_inverse(cells, KZ)
    rows_back = complex_dot(mixed, row_inverse, "cjmk,jx->cxmk")
    rows_back = lax.all_to_all(rows_back, "px", split_axis=2, concat_axis=3, tiled=True)
    columns_back = complex_dot(rows_back, column_inverse, "cxmk,my->cxyk")
    columns_back = lax.all_to_all(columns_back, "py", split_axis=3, concat_axis=4, tiled=True)
    spectral_part = jnp.einsum("cxyk,kz->cxyz", columns_back[0], depth_back[0], precision=highest)
    return spectral_part + jnp.einsum(
        "cxyk,kz->cxyz", columns_back[1], depth_back[1], precision=highest
    )


def spectral_layer(field, spectral, mixing, offsets):
    cells = field.shape[3]
    modes = to_modes(field)
    mixed = mix_modes(modes, spectral)
    pointwise = jnp.einsum("cxyz,co->oxyz", field, mixing, preferred_element_type=jnp.float32)
    spectral_part = from_modes(mixed, cells)
    total = spectral_part + pointwise + offsets[:, None, None, None]
    return jax.nn.gelu(total).astype(jnp.bfloat16)


def on_device(field, spec_fine, mix_fine, bias_fine, spec_coarse, mix_coarse, bias_coarse):
    upper = spectral_layer(field, spec_fine, mix_fine, bias_fine)
    channels, rows_x, rows_y, cells = upper.shape
    blocks = upper.astype(jnp.float32).reshape(
        channels, rows_x // 2, 2, rows_y // 2, 2, cells // 2, 2
    )
    pooled = blocks.mean(axis=(2, 4, 6)).astype(jnp.bfloat16)
    lower = spectral_layer(pooled, spec_coarse, mix_coarse, bias_coarse)
    merged = blocks + lower.astype(jnp.float32)[:, :, None, :, None, :, None]
    return merged.reshape(channels, rows_x, rows_y, cells).astype(jnp.bfloat16)


def solution(mesh):
    return jax.shard_map(
        on_device,
        mesh=mesh,
        in_specs=(
            P(None, "px", "py", None),
            P(None, None, None, None, "px", "py"),
            P(),
            P(),
            P(None, None, None, None, "px", "py"),
            P(),
            P(),
        ),
        out_specs=P(None, "px", "py", None),
        check_vma=False,
    )
```

profile of v0, /device:TPU:1, one launch (start us, length us, event | category | flops | bytes accessed | tf_op | source)
XLA Modules:
  0.0 286.4 jit_solution(122157401921060212)
XLA Ops:
  3.2 4.4 %copy.404 = f32[2,32,16,8,32]{1,3,2,0,4:T(8,128)} copy(f32[2,32,16,8,32]{1,4,3,2,0:T(8,128)S(1)} %convolution_bitcast_fusion) | data formatting | bytes 2097152 | tf_op jit(solution)/shard_map/cxyz,rzk->rcxyk/transpose | solution.py:70
  7.5 4.7 %reshape.614 = f32[16,1,16384]{2,1,0:T(1,128)} reshape(f32[32,2,16,8,32]{4,3,2,1,0:T(8,128)} %bitcast.399) | data formatting | bytes 2097152
  12.3 9.4 %all-to-all-start = ((f32[16,1,16384]{2,1,0:T(1,128)}), f32[16,1,16384]{2,1,0:T(1,128)S(1)}, u32[]{:S(2)}, u32[]{:S(2)}) async-start(f32[16,1,16384]{2,1,0:T(1,128)} %reshape.614), calls=%async_computation | async-start | bytes 2097152 | tf_op jit(solution)/shard_map/all_to_all | solution.py:71
  21.7 16.8 %all-to-all-done = f32[16,1,16384]{2,1,0:T(1,128)S(1)} async-done(((f32[16,1,16384]{2,1,0:T(1,128)}), f32[16,1,16384]{2,1,0:T(1,128)S(1)}, u32[]{:S(2)}, u32[]{:S(2)}) %all-to-all-start) | async-done | bytes 1048608 | tf_op jit(solution)/shard_map/all_to_all | solution.py:71
  54.3 4.9 %all-to-all-start.1 = ((f32[8,1,8192]{2,1,0:T(1,128)}), f32[8,1,8192]{2,1,0:T(1,128)S(1)}, u32[]{:S(2)}, u32[]{:S(2)}) async-start(f32[8,1,8192]{2,1,0:T(1,128)} %reshape.616), calls=%async_computation.1 | async-start | bytes 524288 | tf_op jit(solution)/shard_map/all_to_all | solution.py:73
  59.4 6.3 %all-to-all-done.1 = f32[8,1,8192]{2,1,0:T(1,128)S(1)} async-done(((f32[8,1,8192]{2,1,0:T(1,128)}), f32[8,1,8192]{2,1,0:T(1,128)S(1)}, u32[]{:S(2)}, u32[]{:S(2)}) %all-to-all-start.1) | async-done | bytes 262176 | tf_op jit(solution)/shard_map/all_to_all | solution.py:73
  70.1 11.8 %fusion.3 = (f32[32,4,2,32]{0,2,1,3:T(2,128)S(1)}, f32[32,4,2,32]{0,2,1,3:T(2,128)S(1)}, f32[32,4,2,32]{0,2,1,3:T(2,128)S(1)}, f32[32,4,2,32]{0,2,1,3:T(2,128)S(1)}) fusion(f32[32,4,2,32]{0,2,1,3:T(2,128)S(1)} %copy.301, bf16[2,32,32,32,4,2]{3,5,4,2,1,0:T(2,128)(2,1)} %param.8, f32[32,4,2,32]{0,2,1,3:T(2,128)S(1)} %copy.302), kind=kLoop, calls=%fused_computation.11 | loop fusion | flops 2588672 | bytes 1245184
  84.7 8.9 %all_to_all.120 = f32[8,1,8192]{2,1,0:T(1,128)S(1)} all-to-all(f32[8,1,8192]{2,1,0:T(1,128)S(1)} %reshape.618), channel_id=1, replica_groups=mesh['px'=8,'py'=16] {'px'}, dimensions={0} | all-to-all | bytes 524288 | tf_op jit(solution)/shard_map/all_to_all | solution.py:83
  99.4 4.5 %copy.165 = f32[2,32,16,128,2]{1,4,2,0,3:T(2,128)} copy(f32[2,32,16,128,2]{3,1,4,2,0:T(8,128)S(1)} %pad_maximum_fusion.1) | data formatting | bytes 2097152 | tf_op jit(solution)/shard_map/stack | solution.py:50
  103.9 6.5 %reshape.620 = f32[16,1,16384]{2,1,0:T(1,128)} reshape(f32[128,2,16,2,32]{4,3,2,1,0:T(2,128)} %bitcast.398) | data formatting | bytes 2097152
  110.4 8.2 %all-to-all-start.3 = ((f32[16,1,16384]{2,1,0:T(1,128)}), f32[16,1,16384]{2,1,0:T(1,128)S(1)}, u32[]{:S(2)}, u32[]{:S(2)}) async-start(f32[16,1,16384]{2,1,0:T(1,128)} %reshape.620), calls=%async_computation.3 | async-start | bytes 2097152 | tf_op jit(solution)/shard_map/all_to_all | solution.py:85
  120.9 14.5 %all-to-all-done.3 = f32[16,1,16384]{2,1,0:T(1,128)S(1)} async-done(((f32[16,1,16384]{2,1,0:T(1,128)}), f32[16,1,16384]{2,1,0:T(1,128)S(1)}, u32[]{:S(2)}, u32[]{:S(2)}) %all-to-all-start.3) | async-done | bytes 1048608 | tf_op jit(solution)/shard_map/all_to_all | solution.py:85
  138.7 4.9 %reshape.621 = f32[128,2,16,2,32]{4,3,2,1,0:T(2,128)} reshape(f32[16,16384]{1,0:T(8,128)S(1)} %reduce.19) | data formatting | bytes 2097152
  143.5 4.6 %copy.398 = f32[2,32,16,128,2]{1,3,4,2,0:T(8,128)S(1)} copy(f32[2,32,16,128,2]{1,4,2,0,3:T(2,128)} %bitcast.401) | data formatting | bytes 2097152 | tf_op jit(solution)/shard_map/all_to_all | solution.py:85
  164.8 4.9 %copy.174 = f32[32,16,8,128]{0,3,2,1:T(8,128)} copy(f32[32,16,8,128]{3,2,1,0:T(8,128)S(1)} %fusion.21) | data formatting | bytes 4194304 | tf_op jit(solution)/shard_map/convert_element_type | solution.py:105
  169.7 8.8 %reduce_sum.9 = f32[32,8,4,64]{0,3,2,1:T(8,128)S(1)} reduce(f32[32,8,2,4,2,64,2]{0,6,5,4,3,2,1:T(2,128)} %bitcast.396, f32[]{:T(128)} %constant.94.clone.1), dimensions={2,4,6}, to_apply=%region_0.1 | reduce | flops 458752 | bytes 2359300 | tf_op jit(solution)/shard_map/reduce_sum | solution.py:108
  183.4 13.2 %all_to_all.121 = f32[16,1,4096]{2,1,0:T(1,128)S(1)} all-to-all(f32[16,1,4096]{2,1,0:T(1,128)S(1)} %reshape.622), channel_id=1, replica_groups=mesh['px'=8,'py'=16] {'py'}, dimensions={0} | all-to-all | bytes 524288 | tf_op jit(solution)/shard_map/all_to_all | solution.py:71
  207.4 5.2 %all-to-all-done.5 = f32[8,1,4096]{2,1,0:T(1,128)S(1)} async-done(((f32[8,1,4096]{2,1,0:T(1,128)}), f32[8,1,4096]{2,1,0:T(1,128)S(1)}, u32[]{:S(2)}, u32[]{:S(2)}) %all-to-all-start.5) | async-done | bytes 131104 | tf_op jit(solution)/shard_map/all_to_all | solution.py:73
  215.8 11.8 %fusion.7 = (f32[32,4,2,32]{0,2,1,3:T(2,128)S(1)}, f32[32,4,2,32]{0,2,1,3:T(2,128)S(1)}, f32[32,4,2,32]{0,2,1,3:T(2,128)S(1)}, f32[32,4,2,32]{0,2,1,3:T(2,128)S(1)}) fusion(f32[32,4,2,32]{0,2,1,3:T(2,128)S(1)} %copy.303, bf16[2,32,32,32,4,2]{3,5,4,2,1,0:T(2,128)(2,1)} %param.11, f32[32,4,2,32]{0,2,1,3:T(2,128)S(1)} %copy.304), kind=kLoop, calls=%fused_computation.15 | loop fusion | flops 2588672 | bytes 1245184
  233.8 5.4 %all-to-all-done.6 = f32[8,1,4096]{2,1,0:T(1,128)S(1)} async-done(((f32[8,1,4096]{2,1,0:T(1,128)}), f32[8,1,4096]{2,1,0:T(1,128)S(1)}, u32[]{:S(2)}, u32[]{:S(2)}) %all-to-all-start.6) | async-done | bytes 131104 | tf_op jit(solution)/shard_map/all_to_all | solution.py:83
  247.3 6.0 %all-to-all-start.7 = ((f32[16,1,4096]{2,1,0:T(1,128)}), f32[16,1,4096]{2,1,0:T(1,128)S(1)}, u32[]{:S(2)}, u32[]{:S(2)}) async-start(f32[16,1,4096]{2,1,0:T(1,128)} %reshape.628), calls=%async_computation.7 | async-start | bytes 524288 | tf_op jit(solution)/shard_map/all_to_all | solution.py:85
  253.4 8.8 %all-to-all-done.7 = f32[16,1,4096]{2,1,0:T(1,128)S(1)} async-done(((f32[16,1,4096]{2,1,0:T(1,128)}), f32[16,1,4096]{2,1,0:T(1,128)S(1)}, u32[]{:S(2)}, u32[]{:S(2)}) %all-to-all-start.7) | async-done | bytes 262176 | tf_op jit(solution)/shard_map/all_to_all | solution.py:85
  269.3 7.4 %add.312 = f32[32,8,2,4,2,64,2]{0,6,5,4,3,2,1:T(2,128)} broadcast(f32[32,8,4,64]{0,3,2,1:T(8,128)S(1)} %copy.205), dimensions={0,1,3,5} | broadcast | bytes 2359296 | tf_op jit(solution)/shard_map/add | solution.py:110
  276.7 6.5 %copy.206 = f32[32,16,8,128]{3,2,1,0:T(8,128)} copy(f32[32,16,8,128]{0,3,2,1:T(8,128)} %bitcast.397) | data formatting | bytes 4194304 | tf_op jit(solution)/shard_map/add | solution.py:110
  (148 shorter events, 96.9 us)
Async XLA Ops:
  0.0 118.9 %copy-start = (bf16[32,32]{1,0:T(8,128)(2,1)S(1)}, bf16[32,32]{1,0:T(8,128)(2,1)}, u32[]{:S(2)}) copy-start(bf16[32,32]{1,0:T(8,128)(2,1)} %param.9) | copy-start | bytes 6148
  12.3 26.2 %all-to-all-start = ((f32[16,1,16384]{2,1,0:T(1,128)}), f32[16,1,16384]{2,1,0:T(1,128)S(1)}, u32[]{:S(2)}, u32[]{:S(2)}) async-start(f32[16,1,16384]{2,1,0:T(1,128)} %reshape.614), calls=%async_computation | async-start | bytes 2097152 | tf_op jit(solution)/shard_map/all_to_all | solution.py:71
  54.3 11.4 %all-to-all-start.1 = ((f32[8,1,8192]{2,1,0:T(1,128)}), f32[8,1,8192]{2,1,0:T(1,128)S(1)}, u32[]{:S(2)}, u32[]{:S(2)}) async-start(f32[8,1,8192]{2,1,0:T(1,128)} %reshape.616), calls=%async_computation.1 | async-start | bytes 524288 | tf_op jit(solution)/shard_map/all_to_all | solution.py:73
  110.4 8.5 %copy-start.4 = (bf16[32,16,8,128]{3,2,1,0:T(8,128)(2,1)S(1)}, bf16[32,16,8,128]{3,2,1,0:T(8,128)(2,1)}, u32[]{:S(2)}) copy-start(bf16[32,16,8,128]{3,2,1,0:T(8,128)(2,1)} %param.7) | copy-start | bytes 3145732
  110.4 25.1 %all-to-all-start.3 = ((f32[16,1,16384]{2,1,0:T(1,128)}), f32[16,1,16384]{2,1,0:T(1,128)S(1)}, u32[]{:S(2)}, u32[]{:S(2)}) async-start(f32[16,1,16384]{2,1,0:T(1,128)} %reshape.620), calls=%async_computation.3 | async-start | bytes 2097152 | tf_op jit(solution)/shard_map/all_to_all | solution.py:85
  157.5 3.6 %copy-start.2 = (f32[32,16,8,128]{3,0,2,1:T(8,128)S(1)}, f32[32,16,8,128]{3,0,2,1:T(8,128)}, u32[]{:S(2)}) copy-start(f32[32,16,8,128]{3,0,2,1:T(8,128)} %fusion.43) | copy-start | bytes 6291460
  157.5 3.6 %copy-start.3 = (f32[32,16,8,32]{3,2,1,0:T(8,128)S(1)}, f32[32,16,8,32]{3,2,1,0:T(8,128)}, u32[]{:S(2)}) copy-start(f32[32,16,8,32]{3,2,1,0:T(8,128)} %copy.170) | copy-start | bytes 1572868
  157.5 3.6 %copy-start.7 = (f32[32]{0:T(128)S(1)}, f32[32]{0:T(128)}, u32[]{:S(2)}) copy-start(f32[32]{0:T(128)} %param.10) | copy-start | bytes 388
  180.8 0.7 copy-start.5
  203.9 8.8 %all-to-all-start.5 = ((f32[8,1,4096]{2,1,0:T(1,128)}), f32[8,1,4096]{2,1,0:T(1,128)S(1)}, u32[]{:S(2)}, u32[]{:S(2)}) async-start(f32[8,1,4096]{2,1,0:T(1,128)} %reshape.624), calls=%async_computation.5 | async-start | bytes 262144 | tf_op jit(solution)/shard_map/all_to_all | solution.py:73
  230.3 8.9 %all-to-all-start.6 = ((f32[8,1,4096]{2,1,0:T(1,128)}), f32[8,1,4096]{2,1,0:T(1,128)S(1)}, u32[]{:S(2)}, u32[]{:S(2)}) async-start(f32[8,1,4096]{2,1,0:T(1,128)} %reshape.626), calls=%async_computation.6 | async-start | bytes 262144 | tf_op jit(solution)/shard_map/all_to_all | solution.py:83
  247.3 15.0 %all-to-all-start.7 = ((f32[16,1,4096]{2,1,0:T(1,128)}), f32[16,1,4096]{2,1,0:T(1,128)S(1)}, u32[]{:S(2)}, u32[]{:S(2)}) async-start(f32[16,1,4096]{2,1,0:T(1,128)} %reshape.628), calls=%async_computation.7 | async-start | bytes 524288 | tf_op jit(solution)/shard_map/all_to_all | solution.py:85
  264.6 2.1 copy-start.6
  264.6 2.1 copy-start.8
  264.6 2.1 copy-start.9
  276.7 9.5 %copy-start.1 = (bf16[32,32]{1,0:T(8,128)(2,1)S(1)}, bf16[32,32]{1,0:T(8,128)(2,1)}, u32[]{:S(2)}) copy-start(bf16[32,32]{1,0:T(8,128)(2,1)} %param.9) | copy-start | bytes 6148
where the time goes:
time: 292 us; the launch traced here: 286 us
  local copies, waits for them, and re-layouts  87.3 us (30%)
  waiting for transfers between devices  57 us (20%)
  other arithmetic  51.2 us (18%)
  starting transfers between devices  35.4 us (12%)
  matrix products  32.2 us (11%)
  blocking collectives  22.1 us (8%)
    unnamed x40, local copies, waits for them, and re-layouts  31.8 us
    unnamed x2, other arithmetic  23.5 us
    all_to_all x2, waiting for transfers between devices, from_modes(): lax.all_to_all(columns_back, 'py', split_axis=3, concat_axis=4, tiled=True)  23.4 us
    all_to_all x1, waiting for transfers between devices, to_modes(): depth = lax.all_to_all(depth, 'py', split_axis=4, concat_axis=3, tiled=True)  16.8 us
    all_to_all x2, starting transfers between devices, from_modes(): lax.all_to_all(columns_back, 'py', split_axis=3, concat_axis=4, tiled=True)  14.2 us
    add x2, local copies, waits for them, and re-layouts, on_device(): merged = blocks + lower.astype(jnp.float32)[:, :, None, :, None, :, None]  13.9 us
    all_to_all x1, blocking collectives, to_modes(): depth = lax.all_to_all(depth, 'py', split_axis=4, concat_axis=3, tiled=True)  13.2 us
    all_to_all x2, waiting for transfers between devices, to_modes(): lax.all_to_all(across, 'px', split_axis=3, concat_axis=2, tiled=True)  11.5 us
  transfers between devices with their start and end apart: 6, of which 6 were waited for; matrix products, arithmetic and copies ran while one was open for 1% of the time, Pallas kernels for 0%

commit v1 on v0

v1 whole, which is shorter than its diff:
```python
import functools
import math

import jax
import jax.numpy as jnp
import numpy as np
from jax import lax
from jax.experimental import pallas as pl
from jax.experimental.pallas import tpu as pltpu
from jax.sharding import PartitionSpec as P

C = 32
KEPT = 32
F32 = jnp.float32
BF16 = jnp.bfloat16


def angles(cells, offset):
    windings = np.arange(cells)[:, None] * (np.arange(KEPT)[None, :] - offset) % cells
    return windings.astype(np.float64) * (2.0 * math.pi / cells)


def depth_forward(cells, repeat):
    angle = angles(cells, 0)
    table = np.stack([np.cos(angle), -np.sin(angle)])
    table = table.reshape(2, cells, 16, 2).transpose(1, 2, 0, 3)
    spread = np.zeros((cells, repeat) + table.shape[1:])
    spread[:, 0] = table
    spread = spread.reshape((cells * repeat,) + table.shape[1:])
    result = np.einsum("zprk,hg->hzprkg", spread, np.eye(4))
    return result.reshape(4 * cells * repeat, 256).astype(BF16)


def plane_forward(cells):
    angle = angles(cells, KEPT // 2)
    return np.concatenate([np.cos(angle), -np.sin(angle)], axis=1).T.astype(BF16)


def halves(table):
    high = table.astype(np.float32).astype(BF16)
    low = (table.astype(np.float32) - high.astype(np.float32)).astype(BF16)
    return high, low


def plane_inverse(cells):
    angle = angles(cells, KEPT // 2)
    high, low = halves(np.concatenate([np.cos(angle), np.sin(angle)], axis=1))
    return np.concatenate([high, low], axis=1)


def depth_inverse(cells, repeat):
    angle = angles(cells, 0)
    factor = np.where(np.arange(KEPT) == 0, 1.0, 2.0) / float(cells**3)
    table = np.stack([factor * np.cos(angle), -factor * np.sin(angle)])
    table = np.repeat(table, repeat, axis=1).reshape(2, cells * repeat, 16, 2)
    result = np.einsum("rzpk,hg->prkhgz", table, np.eye(4)).reshape(256, 4 * cells * repeat)
    return np.concatenate(halves(result), axis=0)


def dot(a, b):
    return jnp.dot(a, b, preferred_element_type=F32)


def lanes_of(shape):
    return lax.broadcasted_iota(jnp.int32, shape, len(shape) - 1)


def turn(x):
    width = x.shape[-1]
    real = (lanes_of(x.shape) & 8) == 0
    return jnp.where(real, -pltpu.roll(x, width - 8, 1), pltpu.roll(x, 8, 1))


def swap_blocks(parts):
    parts = list(parts)
    lane = lanes_of(parts[0].shape)
    for step in (1, 2, 4):
        keep = (lane & (16 * step)) == 0
        for low in range(8):
            if low & step == 0:
                a, b = parts[low], parts[low + step]
                parts[low] = jnp.where(keep, a, pltpu.roll(b, 16 * step, 1))
                parts[low + step] = jnp.where(keep, pltpu.roll(a, 128 - 16 * step, 1), b)
    return parts


def spread_groups(product, send, rows):
    def chunk(index, carry):
        at = pl.ds(pl.multiple_of(index * 16, 16), 16)
        for half in range(2):
            parts = swap_blocks([product[g, at, 128 * half : 128 * half + 128] for g in range(8)])
            for b in range(8):
                send[8 * half + b, at, :] = parts[b].astype(BF16)
        return carry

    lax.fori_loop(0, rows // 16, chunk, 0)


def collect_groups(received, spread, rows):
    def chunk(index, carry):
        at = pl.ds(pl.multiple_of(index * 16, 16), 16)
        for half in range(2):
            parts = swap_blocks([received[8 * half + b, at, :].astype(F32) for b in range(8)])
            for g in range(8):
                spread[g, at, 128 * half : 128 * half + 128] = parts[g].astype(BF16)
        return carry

    lax.fori_loop(0, rows // 16, chunk, 0)


def depth_kernel(field, table, send, product):
    for g in range(8):
        rows = jnp.concatenate([field[8 * h + g] for h in range(4)], axis=1)
        product[g] = dot(rows, table[...])
    spread_groups(product, send, 128)


def columns_fine_kernel(received, table, send, lines):
    for pair in range(8):
        block = received[:, 16 * pair : 16 * pair + 16, :].astype(F32).reshape(16, 2, 8, 128)
        data = jnp.concatenate([block[:, e].reshape(128, 128) for e in range(2)], axis=1)
        out = dot(table[...], data.astype(BF16))
        out = out[:KEPT] + turn(out[KEPT:])
        for e in range(2):
            lines[pl.ds(2 * pair + e, KEPT, stride=16), :] = out[:, 128 * e : 128 * e + 128]
    send[...] = lines[...].reshape(8, 64, 128).astype(BF16)


def columns_coarse_kernel(received, table, send, cells, lines):
    cells[...] = received[...].astype(F32).reshape(512, 128)
    data = jnp.concatenate([cells[pl.ds(x, 64, stride=8), :] for x in range(8)], axis=1)
    out = dot(table[...], data.astype(BF16))
    out = out[:KEPT] + turn(out[KEPT:])
    for x in range(8):
        lines[pl.ds(x, KEPT, stride=8), :] = out[:, 128 * x : 128 * x + 128]
    send[...] = lines[...].reshape(8, 32, 128).astype(BF16)


def mix_kernel(received, forward, inverse, weights, send, modes, mixed):
    own = received.shape[2]
    data = received[...].astype(F32)
    data = jnp.concatenate([data[:, m].reshape(8 * own, 128) for m in range(4)], axis=1)
    out = dot(forward[...], data.astype(BF16))
    out = out[:KEPT] + turn(out[KEPT:])
    out = jnp.concatenate([out[:, 128 * m : 128 * m + 128] for m in range(4)], axis=0)
    modes[...] = out.T

    def step(g, sums):
        sums = list(sums)
        base = g * 16
        for h in range(4):
            for k in range(2):
                real = modes[pl.ds(base + 4 * k + h, 1), :]
                imag = modes[pl.ds(base + 8 + 4 * k + h, 1), :]
                w_real = weights[0, 8 * h + g, k].astype(F32)
                w_imag = weights[1, 8 * h + g, k].astype(F32)
                sums[2 * k] = sums[2 * k] + (w_real * real - w_imag * imag)
                sums[2 * k + 1] = sums[2 * k + 1] + (w_real * imag + w_imag * real)
        return tuple(sums)

    sums = lax.fori_loop(0, 8, step, tuple(jnp.zeros((C, 128), F32) for _ in range(4)))
    for k in range(2):
        for r in range(2):
            for h in range(4):
                mixed[pl.ds(8 * r + 4 * k + h, 8, stride=16), :] = sums[2 * k + r][8 * h : 8 * h + 8]
    back = mixed[...].T
    back = jnp.concatenate([back[32 * m : 32 * m + 32] for m in range(4)], axis=1)
    back = jnp.concatenate([back, turn(back)], axis=0).astype(BF16)
    out = dot(inverse[...], jnp.concatenate([back, back], axis=0))
    for m in range(4):
        send[:, m] = out[:, 128 * m : 128 * m + 128].reshape(8, own, 128).astype(BF16)


def back_columns(lines, table, own, first, count):
    data = jnp.concatenate([lines[pl.ds(first + x, KEPT, stride=own), :] for x in range(count)], axis=1)
    data = jnp.concatenate([data, turn(data)], axis=0).astype(BF16)
    return dot(table, jnp.concatenate([data, data], axis=0))


def back_fine_kernel(received, table, send, lines):
    lines[...] = received[...].astype(F32).reshape(512, 128)
    for pair in range(8):
        out = back_columns(lines, table[...], 16, 2 * pair, 2)
        parts = [out[:, 128 * e : 128 * e + 128].reshape(16, 1, 8, 128) for e in range(2)]
        block = jnp.concatenate(parts, axis=1).reshape(16, 16, 128)
        send[:, 16 * pair : 16 * pair + 16, :] = block.astype(BF16)


def back_coarse_kernel(received, table, send, lines, cells):
    lines[...] = received[...].astype(F32).reshape(256, 128)
    out = back_columns(lines, table[...], 8, 0, 8)
    for x in range(8):
        cells[pl.ds(x, 64, stride=8), :] = out[:, 128 * x : 128 * x + 128]
    send[...] = cells[...].reshape(16, 32, 128).astype(BF16)


def channel_map(mixing):
    row = lax.broadcasted_iota(jnp.int32, (512, C), 0)
    channel = lax.broadcasted_iota(jnp.int32, (512, C), 1)
    pick = jnp.where((row >> 4) == channel, 1.0, 0.0).astype(BF16)
    wide = lax.dot_general(pick, mixing, (((1,), (1,)), ((), ())), preferred_element_type=F32)
    wide = lax.dot_general(wide.astype(BF16), pick, (((1,), (1,)), ((), ())), preferred_element_type=F32)
    a = lax.broadcasted_iota(jnp.int32, (512, 512), 0)
    b = lax.broadcasted_iota(jnp.int32, (512, 512), 1)
    return jnp.where(((a ^ b) & 15) == 0, wide, 0.0).astype(BF16)


def pointwise(values, mixing, total, rows):
    blocks = [values[:, 16 * p : 16 * p + 16, :].reshape(512, 128) for p in range(rows // 16)]
    out = dot(channel_map(mixing), jnp.concatenate(blocks, axis=1))
    for p in range(rows // 16):
        total[:, 16 * p : 16 * p + 16, :] = out[:, 128 * p : 128 * p + 128].reshape(C, 16, 128)


def gelu(v):
    inner = v * (0.7978845608028654 + 0.03567740813636141 * (v * v))
    half = 0.5 * v
    return half + half * jnp.tanh(inner)


def upper_kernel(received, table, field, mixing, bias, next_table, upper, pooled, send, spread, total, sums, product):
    pointwise(field, mixing[...], total, 128)
    collect_groups(received, spread, 128)
    even = (lanes_of((64, 128)) & 1) == 0

    def group(g, carry):
        data = spread[g]
        out = dot(jnp.concatenate([data, data], axis=1), table[...])
        for h in range(4):
            o = 8 * h + g
            value = gelu(out[:, 128 * h : 128 * h + 128] + total[o] + bias[o]).astype(BF16)
            upper[o] = value
            value = value.astype(F32).reshape(8, 2, 8, 128)
            value = (value[:, 0] + value[:, 1]).reshape(64, 128)
            value = value + jnp.where(even, pltpu.roll(value, 127, 1), pltpu.roll(value, 1, 1))
            sums[...] = value
            parts = [sums[pl.ds(2 * y, 8, stride=8), :] + sums[pl.ds(2 * y + 1, 8, stride=8), :] for y in range(4)]
            pooled[o] = (jnp.concatenate(parts, axis=0) * 0.125).astype(BF16)
        rows = jnp.concatenate([pooled[8 * h + g] for h in range(4)], axis=1)
        product[g] = dot(rows, next_table[...])
        return carry

    lax.fori_loop(0, 8, group, 0)
    spread_groups(product, send, 32)


def lower_kernel(received, table, pooled, mixing, bias, upper, out_ref, spread, total, sums):
    pointwise(pooled, mixing[...], total, 32)
    collect_groups(received, spread, 32)

    def group(g, carry):
        data = spread[g]
        out = dot(jnp.concatenate([data, data], axis=1), table[...])
        for h in range(4):
            o = 8 * h + g
            value = gelu(out[:, 128 * h : 128 * h + 128] + total[o] + bias[o]).astype(BF16).astype(F32)
            for y in range(4):
                part = value[8 * y : 8 * y + 8]
                sums[pl.ds(2 * y, 8, stride=8), :] = part
                sums[pl.ds(2 * y + 1, 8, stride=8), :] = part
            added = sums[...].reshape(8, 1, 8, 128)
            fine = upper[o].astype(F32).reshape(8, 2, 8, 128)
            out_ref[o] = (fine + added).reshape(128, 128).astype(BF16)
        return carry

    lax.fori_loop(0, 8, group, 0)


def call(kernel, outs, *operands, scratch=(), scalars=()):
    vmem = pl.BlockSpec(memory_space=pltpu.VMEM)
    smem = pl.BlockSpec(memory_space=pltpu.SMEM)
    shapes = [jax.ShapeDtypeStruct(shape, BF16) for shape in outs]
    return pl.pallas_call(
        kernel,
        out_shape=shapes if len(shapes) > 1 else shapes[0],
        in_specs=[smem if i in scalars else vmem for i in range(len(operands))],
        out_specs=[vmem] * len(shapes) if len(shapes) > 1 else vmem,
        scratch_shapes=[pltpu.VMEM(shape, kind) for shape, kind in scratch],
        compiler_params=pltpu.CompilerParams(vmem_limit_bytes=48 << 20),
    )(*operands)


def exchange(x, axis):
    return lax.all_to_all(x, axis, 0, 0, tiled=True)


def lay_out(spectral):
    turned = jnp.transpose(spectral, (0, 1, 5, 2, 4, 3))
    return jnp.concatenate([turned[..., m, :] for m in range(4)], axis=-1)


def on_device(field, spec_fine, mix_fine, bias_fine, spec_coarse, mix_coarse, bias_coarse):
    field = field.reshape(C, 128, 128)
    forward_fine, inverse_fine = jnp.asarray(plane_forward(128)), jnp.asarray(plane_inverse(128))
    forward_coarse, inverse_coarse = jnp.asarray(plane_forward(64)), jnp.asarray(plane_inverse(64))
    weights_fine = lay_out(spec_fine)
    weights_coarse = lay_out(spec_coarse)

    x = call(depth_kernel, [(16, 128, 128)], field, jnp.asarray(depth_forward(128, 1)), scratch=[((8, 128, 256), F32)])
    x = exchange(x, "py")
    x = call(columns_fine_kernel, [(8, 64, 128)], x, forward_fine, scratch=[((512, 128), F32)])
    x = exchange(x, "px").reshape(8, 4, 16, 128)
    mix_scratch = [((128, 128), F32), ((128, 128), F32)]
    x = call(mix_kernel, [(8, 4, 16, 128)], x, forward_fine, inverse_fine, weights_fine, scratch=mix_scratch)
    x = exchange(x.reshape(8, 64, 128), "px")
    x = call(back_fine_kernel, [(16, 128, 128)], x, inverse_fine, scratch=[((512, 128), F32)])
    x = exchange(x, "py")
    upper, pooled, x = call(
        upper_kernel,
        [(C, 128, 128), (C, 32, 128), (16, 32, 128)],
        x,
        jnp.asarray(depth_inverse(128, 1)),
        field,
        mix_fine,
        bias_fine,
        jnp.asarray(depth_forward(64, 2)),
        scratch=[((8, 128, 256), BF16), ((C, 128, 128), F32), ((64, 128), F32), ((8, 32, 256), F32)],
        scalars=(4,),
    )
    x = exchange(x, "py")
    x = call(columns_coarse_kernel, [(8, 32, 128)], x, forward_coarse, scratch=[((512, 128), F32), ((256, 128), F32)])
    x = exchange(x, "px").reshape(8, 4, 8, 128)
    x = call(mix_kernel, [(8, 4, 8, 128)], x, forward_coarse, inverse_coarse, weights_coarse, scratch=mix_scratch)
    x = exchange(x.reshape(8, 32, 128), "px")
    x = call(back_coarse_kernel, [(16, 32, 128)], x, inverse_coarse, scratch=[((256, 128), F32), ((512, 128), F32)])
    x = exchange(x, "py")
    out = call(
        lower_kernel,
        [(C, 128, 128)],
        x,
        jnp.asarray(depth_inverse(64, 2)),
        pooled,
        mix_coarse,
        bias_coarse,
        upper,
        scratch=[((8, 32, 256), BF16), ((C, 32, 128), F32), ((64, 128), F32)],
        scalars=(4,),
    )
    return out.reshape(C, 16, 8, 128)


def solution(mesh):
    return jax.shard_map(
        on_device,
        mesh=mesh,
        in_specs=(
            P(None, "px", "py", None),
            P(None, None, None, None, "px", "py"),
            P(),
            P(),
            P(None, None, None, None, "px", "py"),
            P(),
            P(),
        ),
        out_specs=P(None, "px", "py", None),
        check_vma=False,
    )
```

time: 292 us -> 126 us (0.43); the launches traced: 286 us -> 126 us
  local copies, waits for them, and re-layouts: 87.3 us -> 19.5 us
  other arithmetic: 51.2 us -> 6.43 us
  waiting for transfers between devices: 57 us -> 17.9 us
  matrix products: 32.2 us -> 0 us
  Pallas kernels: 0 us -> 22.4 us
  blocking collectives: 22.1 us -> 30.3 us
  starting transfers between devices: 35.4 us -> 28.8 us
    all_to_all x6 -> x5, waiting for transfers between devices: 57 us -> 17.9 us  [exchange(): return lax.all_to_all(x, axis, 0, 0, tiled=True)]
    dot_general x40 -> x0, matrix products: 32.2 us -> none  [the longest x2 4.75 us: from_modes(): jnp.einsum('cxyk,kz->cxyz', columns_back[1], depth_back[1], precision=hig...]
    unnamed x2 -> x0, other arithmetic: 23.5 us -> none
    pallas_call x0 -> x9, Pallas kernels: none -> 22.4 us  [call(): pl.pallas_call(kernel, out_shape=shapes if len(shapes) > 1 else shapes[0]...]
    unnamed x40 -> x30, local copies, waits for them, and re-layouts: 31.8 us -> 12.1 us
    add x2 -> x0, local copies, waits for them, and re-layouts: 13.9 us -> none  [on_device(): merged = blocks + lower.astype(jnp.float32)[:, :, None, :, None, :, None]]
    all_to_all x8 -> x0, other arithmetic: 13 us -> none  [the longest x2 4.42 us: from_modes(): lax.all_to_all(columns_back, 'py', split_axis=3, concat_axis=4, tiled=True)]
    another operation x6 -> x0, local copies, waits for them, and re-layouts: 9 us -> none  [complex_dot(): return jnp.stack([real, imag])]
  transfers between devices with their start and end apart: 6 -> 5, of which waited for: 6 -> 5; matrix products, arithmetic and copies ran while one was open for 1% -> 18% of each run, Pallas kernels for 0% -> 0%
where the time goes in v1:
time: 126 us
  blocking collectives  30.3 us (24%)
  starting transfers between devices  28.8 us (23%)
  Pallas kernels  22.4 us (18%)
  local copies, waits for them, and re-layouts  19.5 us (15%)
  waiting for transfers between devices  17.9 us (14%)
  other arithmetic  6.43 us (5%)
    all_to_all x3, blocking collectives, exchange(): return lax.all_to_all(x, axis, 0, 0, tiled=True)  30.3 us
    all_to_all x5, starting transfers between devices, exchange(): return lax.all_to_all(x, axis, 0, 0, tiled=True)  28.8 us
    pallas_call x9, Pallas kernels, call(): pl.pallas_call(kernel, out_shape=shapes if len(shapes) > 1 else shapes[0]...  22.4 us
    all_to_all x5, waiting for transfers between devices, exchange(): return lax.all_to_all(x, axis, 0, 0, tiled=True)  17.9 us
    unnamed x30, local copies, waits for them, and re-layouts  12.1 us
    squeeze x2, local copies, waits for them, and re-layouts, lay_out(): return jnp.concatenate([turned[..., m, :] for m in range(4)], axis=-1)  7.4 us
    concatenate x2, other arithmetic, lay_out(): return jnp.concatenate([turned[..., m, :] for m in range(4)], axis=-1)  6.43 us
  transfers between devices with their start and end apart: 5, of which 5 were waited for; matrix products, arithmetic and copies ran while one was open for 18% of the time, Pallas kernels for 0%

profile of v1, /device:TPU:1, one launch (start us, length us, event | category | flops | bytes accessed | tf_op | source)
XLA Modules:
  0.0 125.5 jit_solution(18031568158351710879)
XLA Ops:
  0.0 1.2 copy-done
  2.2 3.2 %shard_map.145 = bf16[16,128,128]{2,1,0:T(8,128)(2,1)} custom-call(bf16[32,128,128]{2,1,0:T(8,128)(2,1)S(1)} %bitcast.28, bf16[512,256]{1,0:T(8,128)(2,1)S(1)} %copy-done.4), custom_call_target="tpu_custom_call" | custom-call | tf_op jit(solution)/shard_map/pallas_call | solution.py:273
  5.3 9.1 %all-to-all-start = ((bf16[16,128,128]{2,1,0:T(8,128)(2,1)}), bf16[16,128,128]{2,1,0:T(8,128)(2,1)S(1)}, u32[]{:S(2)}, u32[]{:S(2)}) async-start(bf16[16,128,128]{2,1,0:T(8,128)(2,1)} %shard_map.145), calls=%async_computation | async-start | bytes 1048576 | tf_op jit(solution)/shard_map/all_to_all | solution.py:284
  14.5 3.4 %copy.21 = bf16[2,32,32,32,4,2]{3,2,5,1,0,4:T(8,128)(2,1)S(1)} copy(bf16[2,32,32,32,4,2]{3,5,4,2,1,0:T(2,128)(2,1)} %param.16) | data formatting | bytes 2097152 | tf_op args[1]
  17.9 2.4 %slice_bitcast_fusion.7 = (bf16[2,32,2,32,32]{4,3,2,1,0:T(8,128)(2,1)S(1)}, bf16[2,32,2,32,32]{4,3,2,1,0:T(8,128)(2,1)S(1)}, bf16[2,32,2,32,32]{4,3,2,1,0:T(8,128)(2,1)}, bf16[2,32,2,32,32]{4,3,2,1,0:T(8,128)(2,1)}) fusion(bf16[2,32,2,32,4,32]{5,3,2,1,0,4:T(8,128)(2,1)S(1)} %bitcast.35), kind=kLoop, calls=%fused_computation.9 | loop fusion | bytes 2097152 | tf_op jit(solution)/shard_map/squeeze | solution.py:289
  20.2 5.4 %all-to-all-done.received = bf16[16,128,128]{2,1,0:T(8,128)(2,1)S(1)} async-done(((bf16[16,128,128]{2,1,0:T(8,128)(2,1)}), bf16[16,128,128]{2,1,0:T(8,128)(2,1)S(1)}, u32[]{:S(2)}, u32[]{:S(2)}) %all-to-all-start) | async-done | bytes 524320 | tf_op jit(solution)/shard_map/all_to_all | solution.py:284
  26.7 4.7 %all-to-all-start.1 = ((bf16[8,64,128]{2,1,0:T(8,128)(2,1)}), bf16[8,64,128]{2,1,0:T(8,128)(2,1)S(1)}, u32[]{:S(2)}, u32[]{:S(2)}) async-start(bf16[8,64,128]{2,1,0:T(8,128)(2,1)} %shard_map.146), calls=%async_computation.1 | async-start | bytes 262144 | tf_op jit(solution)/shard_map/all_to_all | solution.py:284
  31.3 2.9 %pad_maximum_fusion.weights = bf16[2,32,2,32,128]{4,3,2,1,0:T(8,128)(2,1)S(1)} fusion(bf16[2,32,2,32,32]{4,3,2,1,0:T(8,128)(2,1)S(1)} %get-tuple-element.16, bf16[2,32,2,32,32]{4,3,2,1,0:T(8,128)(2,1)} %get-tuple-element.17, bf16[2,32,2,32,32]{4,3,2,1,0:T(8,128)(2,1)} %get-tuple-element.18, bf16[2,32,2,32,32]{4,3,2,1,0:T(8,128)(2,1)S(1)} %get-tuple-element.15), kind=kLoop, calls=%fused_computation.10 | loop fusion | flops 4194304 | bytes 2097152 | tf_op jit(solution)/shard_map/concatenate | solution.py:289
  34.3 2.5 %all-to-all-done.1 = bf16[8,64,128]{2,1,0:T(8,128)(2,1)S(1)} async-done(((bf16[8,64,128]{2,1,0:T(8,128)(2,1)}), bf16[8,64,128]{2,1,0:T(8,128)(2,1)S(1)}, u32[]{:S(2)}, u32[]{:S(2)}) %all-to-all-start.1) | async-done | bytes 131104 | tf_op jit(solution)/shard_map/all_to_all | solution.py:284
  37.9 8.0 %all_to_all.40.received = bf16[8,64,128]{2,1,0:T(8,128)(2,1)S(1)} all-to-all(bf16[8,64,128]{2,1,0:T(8,128)(2,1)S(1)} %bitcast.31), channel_id=1, replica_groups=mesh['px'=8,'py'=16] {'px'}, dimensions={0} | all-to-all | bytes 262144 | tf_op jit(solution)/shard_map/all_to_all | solution.py:284
  45.8 1.2 shard_map.148
  47.0 7.2 %all-to-all-start.3 = ((bf16[16,128,128]{2,1,0:T(8,128)(2,1)}), bf16[16,128,128]{2,1,0:T(8,128)(2,1)S(1)}, u32[]{:S(2)}, u32[]{:S(2)}) async-start(bf16[16,128,128]{2,1,0:T(8,128)(2,1)} %shard_map.148), calls=%async_computation.3 | async-start | bytes 1048576 | tf_op jit(solution)/shard_map/all_to_all | solution.py:284
  54.2 5.5 %copy.20 = bf16[2,32,32,32,4,2]{3,2,5,1,0,4:T(8,128)(2,1)} copy(bf16[2,32,32,32,4,2]{3,5,4,2,1,0:T(2,128)(2,1)} %param.19) | data formatting | bytes 2097152 | tf_op args[4]
  59.7 5.7 %all-to-all-done.3.received = bf16[16,128,128]{2,1,0:T(8,128)(2,1)S(1)} async-done(((bf16[16,128,128]{2,1,0:T(8,128)(2,1)}), bf16[16,128,128]{2,1,0:T(8,128)(2,1)S(1)}, u32[]{:S(2)}, u32[]{:S(2)}) %all-to-all-start.3) | async-done | bytes 524320 | tf_op jit(solution)/shard_map/all_to_all | solution.py:284
  66.4 9.0 %shard_map.149 = (bf16[32,128,128]{2,1,0:T(8,128)(2,1)S(1)}, bf16[32,32,128]{2,1,0:T(8,128)(2,1)S(1)}, bf16[16,32,128]{2,1,0:T(8,128)(2,1)}) custom-call(bf16[16,128,128]{2,1,0:T(8,128)(2,1)S(1)} %all-to-all-done.3.received, bf16[512,512]{1,0:T(8,128)(2,1)S(1)} %copy-done.3, bf16[32,128,128]{2,1,0:T(8,128)(2,1)S(1)} %bitcast.29, ...), custom_call_target="tpu_custom_call" | custom-call | tf_op jit(solution)/shard_map/pallas_call | solution.py:273
  75.5 4.6 %all-to-all-start.4 = ((bf16[16,32,128]{2,1,0:T(8,128)(2,1)}), bf16[16,32,128]{2,1,0:T(8,128)(2,1)S(1)}, u32[]{:S(2)}, u32[]{:S(2)}) async-start(bf16[16,32,128]{2,1,0:T(8,128)(2,1)} %get-tuple-element.8), calls=%async_computation.4 | async-start | bytes 262144 | tf_op jit(solution)/shard_map/all_to_all | solution.py:284
  80.0 5.0 %slice_bitcast_fusion.3 = (bf16[2,32,2,32,32]{4,3,2,1,0:T(8,128)(2,1)}, bf16[2,32,2,32,32]{4,3,2,1,0:T(8,128)(2,1)}, bf16[2,32,2,32,32]{4,3,2,1,0:T(8,128)(2,1)}, bf16[2,32,2,32,32]{4,3,2,1,0:T(8,128)(2,1)}) fusion(bf16[2,32,2,32,4,32]{5,3,2,1,0,4:T(8,128)(2,1)} %bitcast.34), kind=kLoop, calls=%fused_computation.5 | loop fusion | bytes 2097152 | tf_op jit(solution)/shard_map/squeeze | solution.py:289
  85.1 2.7 %all-to-all-done.4.received = bf16[16,32,128]{2,1,0:T(8,128)(2,1)S(1)} async-done(((bf16[16,32,128]{2,1,0:T(8,128)(2,1)}), bf16[16,32,128]{2,1,0:T(8,128)(2,1)S(1)}, u32[]{:S(2)}, u32[]{:S(2)}) %all-to-all-start.4) | async-done | bytes 131104 | tf_op jit(solution)/shard_map/all_to_all | solution.py:284
  88.7 3.3 %all-to-all-start.5 = ((bf16[8,32,128]{2,1,0:T(8,128)(2,1)}), bf16[8,32,128]{2,1,0:T(8,128)(2,1)S(1)}, u32[]{:S(2)}, u32[]{:S(2)}) async-start(bf16[8,32,128]{2,1,0:T(8,128)(2,1)} %shard_map.150), calls=%async_computation.5 | async-start | bytes 131072 | tf_op jit(solution)/shard_map/all_to_all | solution.py:284
  92.1 3.5 %pad_maximum_fusion.1.weights = bf16[2,32,2,32,128]{4,3,2,1,0:T(8,128)(2,1)S(1)} fusion(bf16[2,32,2,32,32]{4,3,2,1,0:T(8,128)(2,1)} %get-tuple-element.12, bf16[2,32,2,32,32]{4,3,2,1,0:T(8,128)(2,1)} %get-tuple-element.13, bf16[2,32,2,32,32]{4,3,2,1,0:T(8,128)(2,1)} %get-tuple-element.14, bf16[2,32,2,32,32]{4,3,2,1,0:T(8,128)(2,1)} %get-tuple-element.11), kind=kLoop, calls=%fused_computation.11 | loop fusion | flops 4194304 | bytes 2097152 | tf_op jit(solution)/shard_map/concatenate | solution.py:289
  95.6 1.5 %all-to-all-done.5 = bf16[8,32,128]{2,1,0:T(8,128)(2,1)S(1)} async-done(((bf16[8,32,128]{2,1,0:T(8,128)(2,1)}), bf16[8,32,128]{2,1,0:T(8,128)(2,1)S(1)}, u32[]{:S(2)}, u32[]{:S(2)}) %all-to-all-start.5) | async-done | bytes 65568 | tf_op jit(solution)/shard_map/all_to_all | solution.py:284
  98.2 8.6 %all_to_all.41.received = bf16[8,32,128]{2,1,0:T(8,128)(2,1)S(1)} all-to-all(bf16[8,32,128]{2,1,0:T(8,128)(2,1)S(1)} %bitcast.33), channel_id=1, replica_groups=mesh['px'=8,'py'=16] {'px'}, dimensions={0} | all-to-all | bytes 131072 | tf_op jit(solution)/shard_map/all_to_all | solution.py:284
  107.1 13.8 %all_to_all.42.received = bf16[16,32,128]{2,1,0:T(8,128)(2,1)S(1)} all-to-all(bf16[16,32,128]{2,1,0:T(8,128)(2,1)S(1)} %shard_map.152), channel_id=1, replica_groups=mesh['px'=8,'py'=16] {'py'}, dimensions={0} | all-to-all | bytes 262144 | tf_op jit(solution)/shard_map/all_to_all | solution.py:284
  120.9 4.6 %shard_map.153 = bf16[32,128,128]{2,1,0:T(8,128)(2,1)} custom-call(bf16[16,32,128]{2,1,0:T(8,128)(2,1)S(1)} %all_to_all.42.received, bf16[512,512]{1,0:T(8,128)(2,1)S(1)} %copy-done.2, bf16[32,32,128]{2,1,0:T(8,128)(2,1)S(1)} %get-tuple-element.9.pooled, bf16[32,32]{1,0:T(8,128)(2,1)S(1)} %copy-done.10, f32[32]{0:T(128)S(1)} %copy-done.12, ...), custom_call_target="tpu_custom_call" | custom-call | tf_op jit(solution)/shard_map/pallas_call | solution.py:273
  (32 shorter events, 6.4 us)
Async XLA Ops:
  0.0 1.2 copy-start
  1.2 0.9 copy-start.4
  5.3 20.3 %all-to-all-start = ((bf16[16,128,128]{2,1,0:T(8,128)(2,1)}), bf16[16,128,128]{2,1,0:T(8,128)(2,1)S(1)}, u32[]{:S(2)}, u32[]{:S(2)}) async-start(bf16[16,128,128]{2,1,0:T(8,128)(2,1)} %shard_map.145), calls=%async_computation | async-start | bytes 1048576 | tf_op jit(solution)/shard_map/all_to_all | solution.py:284
  17.9 7.8 %copy-start.9 = (bf16[64,128]{1,0:T(8,128)(2,1)S(1)}, bf16[64,128]{1,0:T(8,128)(2,1)}, u32[]{:S(2)}) copy-start(bf16[64,128]{1,0:T(8,128)(2,1)} %constant.16.clone.table.forward) | copy-start | bytes 49156
  26.7 10.1 %all-to-all-start.1 = ((bf16[8,64,128]{2,1,0:T(8,128)(2,1)}), bf16[8,64,128]{2,1,0:T(8,128)(2,1)S(1)}, u32[]{:S(2)}, u32[]{:S(2)}) async-start(bf16[8,64,128]{2,1,0:T(8,128)(2,1)} %shard_map.146), calls=%async_computation.1 | async-start | bytes 262144 | tf_op jit(solution)/shard_map/all_to_all | solution.py:284
  31.3 5.4 %copy-start.6 = (bf16[128,128]{1,0:T(8,128)(2,1)S(1)}, bf16[128,128]{1,0:T(8,128)(2,1)}, u32[]{:S(2)}) copy-start(bf16[128,128]{1,0:T(8,128)(2,1)} %constant.17.clone.inverse.table) | copy-start | bytes 98308
  47.0 18.4 %all-to-all-start.3 = ((bf16[16,128,128]{2,1,0:T(8,128)(2,1)}), bf16[16,128,128]{2,1,0:T(8,128)(2,1)S(1)}, u32[]{:S(2)}, u32[]{:S(2)}) async-start(bf16[16,128,128]{2,1,0:T(8,128)(2,1)} %shard_map.148), calls=%async_computation.3 | async-start | bytes 1048576 | tf_op jit(solution)/shard_map/all_to_all | solution.py:284
  54.2 11.3 %copy-start.1 = (bf16[32,16,8,128]{3,2,1,0:T(8,128)(2,1)S(1)}, bf16[32,16,8,128]{3,2,1,0:T(8,128)(2,1)}, u32[]{:S(2)}) copy-start(bf16[32,16,8,128]{3,2,1,0:T(8,128)(2,1)} %param.15) | copy-start | bytes 3145732
  54.2 11.3 %copy-start.3 = (bf16[512,512]{1,0:T(8,128)(2,1)S(1)}, bf16[512,512]{1,0:T(8,128)(2,1)}, u32[]{:S(2)}) copy-start(bf16[512,512]{1,0:T(8,128)(2,1)} %constant.21.clone.table) | copy-start | bytes 1572868
  54.2 11.2 %copy-start.11 = (bf16[32,32]{1,0:T(8,128)(2,1)S(1)}, bf16[32,32]{1,0:T(8,128)(2,1)}, u32[]{:S(2)}) copy-start(bf16[32,32]{1,0:T(8,128)(2,1)} %mixing.2) | copy-start | bytes 6148
  54.2 11.2 %copy-start.13 = (f32[32]{0:T(128)S(1)}, f32[32]{0:T(128)}, u32[]{:S(2)}) copy-start(f32[32]{0:T(128)} %bias.2) | copy-start | bytes 388
  65.5 1.0 copy-start.5
  75.5 12.3 %all-to-all-start.4 = ((bf16[16,32,128]{2,1,0:T(8,128)(2,1)}), bf16[16,32,128]{2,1,0:T(8,128)(2,1)S(1)}, u32[]{:S(2)}, u32[]{:S(2)}) async-start(bf16[16,32,128]{2,1,0:T(8,128)(2,1)} %get-tuple-element.8), calls=%async_computation.4 | async-start | bytes 262144 | tf_op jit(solution)/shard_map/all_to_all | solution.py:284
  80.0 7.7 %copy-start.8 = (bf16[64,64]{1,0:T(8,128)(2,1)S(1)}, bf16[64,64]{1,0:T(8,128)(2,1)}, u32[]{:S(2)}) copy-start(bf16[64,64]{1,0:T(8,128)(2,1)} %constant.18.clone.table.forward) | copy-start | bytes 24580
  88.7 8.5 %all-to-all-start.5 = ((bf16[8,32,128]{2,1,0:T(8,128)(2,1)}), bf16[8,32,128]{2,1,0:T(8,128)(2,1)S(1)}, u32[]{:S(2)}, u32[]{:S(2)}) async-start(bf16[8,32,128]{2,1,0:T(8,128)(2,1)} %shard_map.150), calls=%async_computation.5 | async-start | bytes 131072 | tf_op jit(solution)/shard_map/all_to_all | solution.py:284
  92.0 5.1 %copy-start.7 = (bf16[64,128]{1,0:T(8,128)(2,1)S(1)}, bf16[64,128]{1,0:T(8,128)(2,1)}, u32[]{:S(2)}) copy-start(bf16[64,128]{1,0:T(8,128)(2,1)} %constant.19.clone.inverse.table) | copy-start | bytes 49156
  92.1 28.9 %copy-start.10 = (bf16[32,32]{1,0:T(8,128)(2,1)S(1)}, bf16[32,32]{1,0:T(8,128)(2,1)}, u32[]{:S(2)}) copy-start(bf16[32,32]{1,0:T(8,128)(2,1)} %mixing.3) | copy-start | bytes 6148
  92.1 28.8 %copy-start.12 = (f32[32]{0:T(128)S(1)}, f32[32]{0:T(128)}, u32[]{:S(2)}) copy-start(f32[32]{0:T(128)} %bias.3) | copy-start | bytes 388
  95.6 25.3 %copy-start.2 = (bf16[512,512]{1,0:T(8,128)(2,1)S(1)}, bf16[512,512]{1,0:T(8,128)(2,1)}, u32[]{:S(2)}) copy-start(bf16[512,512]{1,0:T(8,128)(2,1)} %constant.23.clone.table) | copy-start | bytes 1572868

commit v2 on v1

--- a/solution.py
+++ b/solution.py
@@ -54,7 +54,7 @@
     table = np.stack([factor * np.cos(angle), -factor * np.sin(angle)])
     table = np.repeat(table, repeat, axis=1).reshape(2, cells * repeat, 16, 2)
     result = np.einsum("rzpk,hg->prkhgz", table, np.eye(4)).reshape(256, 4 * cells * repeat)
-    return np.concatenate(halves(result), axis=0)
+    return result.astype(BF16)
 
 
 def dot(a, b):
@@ -108,9 +108,16 @@
     lax.fori_loop(0, rows // 16, chunk, 0)
 
 
-def depth_kernel(field, table, send, product):
+def depth_kernel(field, table_ref, send, values, table, product, arrived):
+    table_copy = pltpu.make_async_copy(table_ref, table, arrived.at[8])
+    table_copy.start()
+    copies = [pltpu.make_async_copy(field.at[:, g], values.at[g], arrived.at[g]) for g in range(8)]
+    for copy in copies:
+        copy.start()
+    table_copy.wait()
     for g in range(8):
-        rows = jnp.concatenate([field[8 * h + g] for h in range(4)], axis=1)
+        copies[g].wait()
+        rows = jnp.concatenate([values[g, h] for h in range(4)], axis=1)
         product[g] = dot(rows, table[...])
     spread_groups(product, send, 128)
 
@@ -205,11 +212,13 @@
     return jnp.where(((a ^ b) & 15) == 0, wide, 0.0).astype(BF16)
 
 
-def pointwise(values, mixing, total, rows):
-    blocks = [values[:, 16 * p : 16 * p + 16, :].reshape(512, 128) for p in range(rows // 16)]
-    out = dot(channel_map(mixing), jnp.concatenate(blocks, axis=1))
-    for p in range(rows // 16):
-        total[:, 16 * p : 16 * p + 16, :] = out[:, 128 * p : 128 * p + 128].reshape(C, 16, 128)
+def pointwise_kernel(field, mix_fine, bias, mix_coarse, total, map_coarse):
+    channels = channel_map(mix_fine[...])
+    for p in range(8):
+        out = dot(channels, field[:, 16 * p : 16 * p + 16, :].reshape(512, 128)).reshape(C, 16, 128)
+        for o in range(C):
+            total[o, 16 * p : 16 * p + 16, :] = out[o] + bias[o]
+    map_coarse[...] = channel_map(mix_coarse[...])
 
 
 def gelu(v):
@@ -218,65 +227,66 @@
     return half + half * jnp.tanh(inner)
 
 
-def upper_kernel(received, table, field, mixing, bias, next_table, upper, pooled, send, spread, total, sums, product):
-    pointwise(field, mixing[...], total, 128)
+def upper_kernel(received, table, total, next_table, upper, pooled, send, spread, sums, product):
     collect_groups(received, spread, 128)
     even = (lanes_of((64, 128)) & 1) == 0
-
-    def group(g, carry):
-        data = spread[g]
-        out = dot(jnp.concatenate([data, data], axis=1), table[...])
+    for g in range(8):
+        out = dot(spread[g], table[...])
         for h in range(4):
             o = 8 * h + g
-            value = gelu(out[:, 128 * h : 128 * h + 128] + total[o] + bias[o]).astype(BF16)
+            value = gelu(out[:, 128 * h : 128 * h + 128] + total[o]).astype(BF16)
             upper[o] = value
             value = value.astype(F32).reshape(8, 2, 8, 128)
             value = (value[:, 0] + value[:, 1]).reshape(64, 128)
-            value = value + jnp.where(even, pltpu.roll(value, 127, 1), pltpu.roll(value, 1, 1))
-            sums[...] = value
-            parts = [sums[pl.ds(2 * y, 8, stride=8), :] + sums[pl.ds(2 * y + 1, 8, stride=8), :] for y in range(4)]
-            pooled[o] = (jnp.concatenate(parts, axis=0) * 0.125).astype(BF16)
+            sums[o] = value + jnp.where(even, pltpu.roll(value, 127, 1), pltpu.roll(value, 1, 1))
+    for o in range(C):
+        parts = [sums[o, pl.ds(2 * y, 8, stride=8), :] + sums[o, pl.ds(2 * y + 1, 8, stride=8), :] for y in range(4)]
+        pooled[o] = (jnp.concatenate(parts, axis=0) * 0.125).astype(BF16)
+    for g in range(8):
         rows = jnp.concatenate([pooled[8 * h + g] for h in range(4)], axis=1)
         product[g] = dot(rows, next_table[...])
-        return carry
-
-    lax.fori_loop(0, 8, group, 0)
     spread_groups(product, send, 32)
 
 
-def lower_kernel(received, table, pooled, mixing, bias, upper, out_ref, spread, total, sums):
-    pointwise(pooled, mixing[...], total, 32)
+def lower_kernel(received, table, pooled, channels, bias, upper, out_ref, spread, total, sums, merged, left):
+    blocks = [pooled[:, 16 * p : 16 * p + 16, :].reshape(512, 128) for p in range(2)]
+    own = dot(channels[...], jnp.concatenate(blocks, axis=1))
+    for p in range(2):
+        total[:, 16 * p : 16 * p + 16, :] = own[:, 128 * p : 128 * p + 128].reshape(C, 16, 128)
     collect_groups(received, spread, 32)
-
-    def group(g, carry):
-        data = spread[g]
-        out = dot(jnp.concatenate([data, data], axis=1), table[...])
+    copies = [pltpu.make_async_copy(merged.at[g], out_ref.at[:, g], left.at[g]) for g in range(8)]
+    for g in range(8):
+        out = dot(spread[g], table[...])
         for h in range(4):
             o = 8 * h + g
             value = gelu(out[:, 128 * h : 128 * h + 128] + total[o] + bias[o]).astype(BF16).astype(F32)
             for y in range(4):
                 part = value[8 * y : 8 * y + 8]
-                sums[pl.ds(2 * y, 8, stride=8), :] = part
-                sums[pl.ds(2 * y + 1, 8, stride=8), :] = part
-            added = sums[...].reshape(8, 1, 8, 128)
+                sums[o, pl.ds(2 * y, 8, stride=8), :] = part
+                sums[o, pl.ds(2 * y + 1, 8, stride=8), :] = part
+            added = sums[o].reshape(8, 1, 8, 128)
             fine = upper[o].astype(F32).reshape(8, 2, 8, 128)
-            out_ref[o] = (fine + added).reshape(128, 128).astype(BF16)
-        return carry
-
-    lax.fori_loop(0, 8, group, 0)
-
-
-def call(kernel, outs, *operands, scratch=(), scalars=()):
-    vmem = pl.BlockSpec(memory_space=pltpu.VMEM)
-    smem = pl.BlockSpec(memory_space=pltpu.SMEM)
-    shapes = [jax.ShapeDtypeStruct(shape, BF16) for shape in outs]
+            merged[g, h] = (fine + added).reshape(128, 128).astype(BF16)
+        copies[g].start()
+    for copy in copies:
+        copy.wait()
+
+
+VMEM = pl.BlockSpec(memory_space=pltpu.VMEM)
+SMEM = pl.BlockSpec(memory_space=pltpu.SMEM)
+HBM = pl.BlockSpec(memory_space=pltpu.HBM)
+
+
+def call(kernel, outs, *operands, scratch=(), specs=None, out_specs=None, limit=8):
+    shapes = [jax.ShapeDtypeStruct(shape, kind) for shape, kind in outs]
+    out_specs = out_specs or [VMEM] * len(shapes)
     return pl.pallas_call(
         kernel,
         out_shape=shapes if len(shapes) > 1 else shapes[0],
-        in_specs=[smem if i in scalars else vmem for i in range(len(operands))],
-        out_specs=[vmem] * len(shapes) if len(shapes) > 1 else vmem,
-        scratch_shapes=[pltpu.VMEM(shape, kind) for shape, kind in scratch],
-        compiler_params=pltpu.CompilerParams(vmem_limit_bytes=48 << 20),
+        in_specs=specs or [VMEM] * len(operands),
+        out_specs=out_specs if len(shapes) > 1 else out_specs[0],
+        scratch_shapes=[pltpu.VMEM(*s) if isinstance(s, tuple) else s for s in scratch],
+        compiler_params=pltpu.CompilerParams(vmem_limit_bytes=limit << 20),
     )(*operands)
 
 
@@ -285,56 +295,87 @@
 
 
 def lay_out(spectral):
-    turned = jnp.transpose(spectral, (0, 1, 5, 2, 4, 3))
-    return jnp.concatenate([turned[..., m, :] for m in range(4)], axis=-1)
+    place = jnp.asarray(np.eye(128).reshape(4, 32, 128).astype(BF16))
+    return jnp.einsum("riojmk,mjl->rikol", spectral, place, preferred_element_type=BF16)
 
 
 def on_device(field, spec_fine, mix_fine, bias_fine, spec_coarse, mix_coarse, bias_coarse):
     field = field.reshape(C, 128, 128)
     forward_fine, inverse_fine = jnp.asarray(plane_forward(128)), jnp.asarray(plane_inverse(128))
     forward_coarse, inverse_coarse = jnp.asarray(plane_forward(64)), jnp.asarray(plane_inverse(64))
+
+    x = call(
+        depth_kernel,
+        [((16, 128, 128), BF16)],
+        field.reshape(4, 8, 128, 128),
+        jnp.asarray(depth_forward(128, 1)),
+        specs=[HBM, HBM],
+        scratch=[
+            ((8, 4, 128, 128), BF16),
+            ((512, 256), BF16),
+            ((8, 128, 256), F32),
+            pltpu.SemaphoreType.DMA((9,)),
+        ],
+    )
+    x = exchange(x, "py")
     weights_fine = lay_out(spec_fine)
     weights_coarse = lay_out(spec_coarse)
-
-    x = call(depth_kernel, [(16, 128, 128)], field, jnp.asarray(depth_forward(128, 1)), scratch=[((8, 128, 256), F32)])
-    x = exchange(x, "py")
-    x = call(columns_fine_kernel, [(8, 64, 128)], x, forward_fine, scratch=[((512, 128), F32)])
+    total, map_coarse = call(
+        pointwise_kernel,
+        [((C, 128, 128), F32), ((512, 512), BF16)],
+        field,
+        mix_fine,
+        bias_fine,
+        mix_coarse,
+        specs=[VMEM, VMEM, SMEM, VMEM],
+    )
+    x, weights_fine, weights_coarse, total, map_coarse = lax.optimization_barrier(
+        (x, weights_fine, weights_coarse, total, map_coarse)
+    )
+    x = call(columns_fine_kernel, [((8, 64, 128), BF16)], x, forward_fine, scratch=[((512, 128), F32)])
     x = exchange(x, "px").reshape(8, 4, 16, 128)
     mix_scratch = [((128, 128), F32), ((128, 128), F32)]
-    x = call(mix_kernel, [(8, 4, 16, 128)], x, forward_fine, inverse_fine, weights_fine, scratch=mix_scratch)
+    x = call(mix_kernel, [((8, 4, 16, 128), BF16)], x, forward_fine, inverse_fine, weights_fine, scratch=mix_scratch)
     x = exchange(x.reshape(8, 64, 128), "px")
-    x = call(back_fine_kernel, [(16, 128, 128)], x, inverse_fine, scratch=[((512, 128), F32)])
+    x = call(back_fine_kernel, [((16, 128, 128), BF16)], x, inverse_fine, scratch=[((512, 128), F32)])
     x = exchange(x, "py")
     upper, pooled, x = call(
         upper_kernel,
-        [(C, 128, 128), (C, 32, 128), (16, 32, 128)],
+        [((C, 128, 128), BF16), ((C, 32, 128), BF16), ((16, 32, 128), BF16)],
         x,
         jnp.asarray(depth_inverse(128, 1)),
-        field,
-        mix_fine,
-        bias_fine,
+        total,
         jnp.asarray(depth_forward(64, 2)),
-        scratch=[((8, 128, 256), BF16), ((C, 128, 128), F32), ((64, 128), F32), ((8, 32, 256), F32)],
-        scalars=(4,),
+        scratch=[((8, 128, 256), BF16), ((C, 64, 128), F32), ((8, 32, 256), F32)],
+        limit=12,
     )
     x = exchange(x, "py")
-    x = call(columns_coarse_kernel, [(8, 32, 128)], x, forward_coarse, scratch=[((512, 128), F32), ((256, 128), F32)])
+    scratch = [((512, 128), F32), ((256, 128), F32)]
+    x = call(columns_coarse_kernel, [((8, 32, 128), BF16)], x, forward_coarse, scratch=scratch)
     x = exchange(x, "px").reshape(8, 4, 8, 128)
-    x = call(mix_kernel, [(8, 4, 8, 128)], x, forward_coarse, inverse_coarse, weights_coarse, scratch=mix_scratch)
+    x = call(mix_kernel, [((8, 4, 8, 128), BF16)], x, forward_coarse, inverse_coarse, weights_coarse, scratch=mix_scratch)
     x = exchange(x.reshape(8, 32, 128), "px")
-    x = call(back_coarse_kernel, [(16, 32, 128)], x, inverse_coarse, scratch=[((256, 128), F32), ((512, 128), F32)])
+    x = call(back_coarse_kernel, [((16, 32, 128), BF16)], x, inverse_coarse, scratch=scratch[::-1])
     x = exchange(x, "py")
     out = call(
         lower_kernel,
-        [(C, 128, 128)],
+        [((4, 8, 128, 128), BF16)],
         x,
         jnp.asarray(depth_inverse(64, 2)),
         pooled,
-        mix_coarse,
+        map_coarse,
         bias_coarse,
         upper,
-        scratch=[((8, 32, 256), BF16), ((C, 32, 128), F32), ((64, 128), F32)],
-        scalars=(4,),
+        specs=[VMEM, VMEM, VMEM, VMEM, SMEM, VMEM],
+        out_specs=[HBM],
+        scratch=[
+            ((8, 32, 256), BF16),
+            ((C, 32, 128), F32),
+            ((C, 64, 128), F32),
+            ((8, 4, 128, 128), BF16),
+            pltpu.SemaphoreType.DMA((8,)),
+        ],
+        limit=12,
     )
     return out.reshape(C, 16, 8, 128)
 

time: 126 us -> 117 us (0.929)
  blocking collectives: 30.3 us -> 76.5 us
  starting transfers between devices: 28.8 us -> 9.13 us
  waiting for transfers between devices: 17.9 us -> 2.21 us
  local copies, waits for them, and re-layouts: 19.5 us -> 4.26 us
  other arithmetic: 6.43 us -> 0 us
  matrix products: 0 us -> 5.77 us
  Pallas kernels: 22.4 us -> 18.8 us
    all_to_all x3 -> x7, blocking collectives: 30.3 us -> 76.5 us  [exchange(): return lax.all_to_all(x, axis, 0, 0, tiled=True)]
    all_to_all x5 -> x1, starting transfers between devices: 28.8 us -> 9.13 us  [exchange(): return lax.all_to_all(x, axis, 0, 0, tiled=True)]
    all_to_all x5 -> x1, waiting for transfers between devices: 17.9 us -> 2.21 us  [exchange(): return lax.all_to_all(x, axis, 0, 0, tiled=True)]
    unnamed x30 -> x38, local copies, waits for them, and re-layouts: 12.1 us -> 4.26 us
    squeeze x2 -> x0, local copies, waits for them, and re-layouts: 7.4 us -> none  [lay_out(): return jnp.concatenate([turned[..., m, :] for m in range(4)], axis=-1)]
    concatenate x2 -> x0, other arithmetic: 6.43 us -> none  [lay_out(): return jnp.concatenate([turned[..., m, :] for m in range(4)], axis=-1)]
    dot_general x0 -> x2, matrix products: none -> 5.77 us  [lay_out(): jnp.einsum('riojmk,mjl->rikol', spectral, place, preferred_element_type=B...]
    pallas_call x9 -> x10, Pallas kernels: 22.4 us -> 18.8 us  [call(): pl.pallas_call(kernel, out_shape=shapes if len(shapes) > 1 else shapes[0]...]
  transfers between devices with their start and end apart: 5 -> 1, of which waited for: 5 -> 1; matrix products, arithmetic and copies ran while one was open for 18% -> 5% of each run, Pallas kernels for 0% -> 2%
where the time goes in v2:
time: 117 us
  blocking collectives  76.5 us (65%)
  Pallas kernels  18.8 us (16%)
  starting transfers between devices  9.13 us (8%)
  matrix products  5.77 us (5%)
  local copies, waits for them, and re-layouts  4.26 us (4%)
  waiting for transfers between devices  2.21 us (2%)
    all_to_all x7, blocking collectives, exchange(): return lax.all_to_all(x, axis, 0, 0, tiled=True)  76.5 us
    pallas_call x10, Pallas kernels, call(): pl.pallas_call(kernel, out_shape=shapes if len(shapes) > 1 else shapes[0]...  18.8 us
    all_to_all x1, starting transfers between devices, exchange(): return lax.all_to_all(x, axis, 0, 0, tiled=True)  9.13 us
    dot_general x2, matrix products, lay_out(): jnp.einsum('riojmk,mjl->rikol', spectral, place, preferred_element_type=B...  5.77 us
    unnamed x38, local copies, waits for them, and re-layouts  4.26 us
  transfers between devices with their start and end apart: 1, of which 1 were waited for; matrix products, arithmetic and copies ran while one was open for 5% of the time, Pallas kernels for 2%

profile of v2, /device:TPU:1, one launch (start us, length us, event | category | flops | bytes accessed | tf_op | source)
XLA Modules:
  0.0 116.8 jit_solution(2012862731368714027)
XLA Ops:
  0.0 1.2 %copy-done = bf16[32,16,8,128]{3,2,1,0:T(8,128)(2,1)S(1)} copy-done((bf16[32,16,8,128]{3,2,1,0:T(8,128)(2,1)S(1)}, bf16[32,16,8,128]{3,2,1,0:T(8,128)(2,1)}, u32[]{:S(2)}) %copy-start) | copy-done | bytes 1048600
  1.2 0.9 copy-done.7
  2.2 4.9 %shard_map.163 = bf16[16,128,128]{2,1,0:T(8,128)(2,1)} custom-call(bf16[4,8,128,128]{3,2,1,0:T(8,128)(2,1)S(1)} %bitcast.22, bf16[512,256]{1,0:T(8,128)(2,1)S(1)} %copy-done.7), custom_call_target="tpu_custom_call" | custom-call | tf_op jit(solution)/shard_map/pallas_call | solution.py:283
  7.1 9.1 %all-to-all-start = ((bf16[16,128,128]{2,1,0:T(8,128)(2,1)}), bf16[16,128,128]{2,1,0:T(8,128)(2,1)}, u32[]{:S(2)}, u32[]{:S(2)}) async-start(bf16[16,128,128]{2,1,0:T(8,128)(2,1)} %shard_map.163), calls=%async_computation | async-start | bytes 1048576 | tf_op jit(solution)/shard_map/all_to_all | solution.py:294
  16.2 4.6 %fusion.4.weights = bf16[2,32,2,32,128]{4,3,2,1,0:T(8,128)(2,1)} fusion(bf16[4,32,128,1,1,1]{2,1,0,5,4,3:T(8,128)(2,1)} %constant.30, bf16[2,32,32,32,4,2]{3,5,4,2,1,0:T(2,128)(2,1)} %param.18), kind=kOutput, calls=%fused_computation.4 | convolution fusion | flops 134217728 | bytes 2129920 | tf_op jit(solution)/shard_map/riojmk,mjl->rikol/dot_general | solution.py:299
  20.8 2.4 %shard_map.164 = (f32[32,128,128]{2,1,0:T(8,128)S(1)}, bf16[512,512]{1,0:T(8,128)(2,1)S(1)}) custom-call(bf16[32,128,128]{2,1,0:T(8,128)(2,1)S(1)} %bitcast.23, bf16[32,32]{1,0:T(8,128)(2,1)S(1)} %copy-done.13, f32[32]{0:T(128)S(1)} %copy-done.15, bf16[32,32]{1,0:T(8,128)(2,1)S(1)} %copy-done.14), custom_call_target="tpu_custom_call" | custom-call | tf_op jit(solution)/shard_map/pallas_call | solution.py:283
  23.3 0.8 copy-done.3
  24.1 1.2 %fusion.7.weights = bf16[2,32,2,32,128]{4,3,2,1,0:T(8,128)(2,1)S(1)} fusion(bf16[4,32,128,1,1,1]{2,1,0,5,4,3:T(8,128)(2,1)S(1)} %copy-done.18, bf16[2,32,32,32,4,2]{3,5,4,2,1,0:T(2,128)(2,1)S(1)} %copy-done.17), kind=kOutput, calls=%fused_computation.5 | convolution fusion | flops 134217728 | bytes 2129920 | tf_op jit(solution)/shard_map/riojmk,mjl->rikol/dot_general | solution.py:299
  25.3 2.2 %all-to-all-done.received = bf16[16,128,128]{2,1,0:T(8,128)(2,1)} async-done(((bf16[16,128,128]{2,1,0:T(8,128)(2,1)}), bf16[16,128,128]{2,1,0:T(8,128)(2,1)}, u32[]{:S(2)}, u32[]{:S(2)}) %all-to-all-start) | async-done | bytes 524320 | tf_op jit(solution)/shard_map/all_to_all | solution.py:294
  27.5 1.5 %shard_map.165 = bf16[8,64,128]{2,1,0:T(8,128)(2,1)S(1)} custom-call(bf16[16,128,128]{2,1,0:T(8,128)(2,1)} %all-to-all-done.received, bf16[64,128]{1,0:T(8,128)(2,1)S(1)} %copy-done.12), custom_call_target="tpu_custom_call" | custom-call | tf_op jit(solution)/shard_map/pallas_call | solution.py:283
  29.0 9.9 %all_to_all.40 = bf16[8,64,128]{2,1,0:T(8,128)(2,1)S(1)} all-to-all(bf16[8,64,128]{2,1,0:T(8,128)(2,1)S(1)} %shard_map.165), channel_id=1, replica_groups=mesh['px'=8,'py'=16] {'px'}, dimensions={0} | all-to-all | bytes 262144 | tf_op jit(solution)/shard_map/all_to_all | solution.py:294
  38.9 1.2 %copy-done.2 = bf16[2,32,2,32,128]{4,3,2,1,0:T(8,128)(2,1)S(1)} copy-done((bf16[2,32,2,32,128]{4,3,2,1,0:T(8,128)(2,1)S(1)}, bf16[2,32,2,32,128]{4,3,2,1,0:T(8,128)(2,1)}, u32[]{:S(2)}) %copy-start.2) | copy-done | bytes 1048600
  40.1 1.1 shard_map.166
  41.2 8.0 %all_to_all.41.received = bf16[8,64,128]{2,1,0:T(8,128)(2,1)S(1)} all-to-all(bf16[8,64,128]{2,1,0:T(8,128)(2,1)S(1)} %bitcast.25), channel_id=1, replica_groups=mesh['px'=8,'py'=16] {'px'}, dimensions={0} | all-to-all | bytes 262144 | tf_op jit(solution)/shard_map/all_to_all | solution.py:294
  49.2 0.4 shard_map.167
  49.6 19.2 %all_to_all.42.received = bf16[16,128,128]{2,1,0:T(8,128)(2,1)S(1)} all-to-all(bf16[16,128,128]{2,1,0:T(8,128)(2,1)S(1)} %shard_map.167), channel_id=1, replica_groups=mesh['px'=8,'py'=16] {'py'}, dimensions={0} | all-to-all | bytes 1048576 | tf_op jit(solution)/shard_map/all_to_all | solution.py:294
  68.8 3.9 %shard_map.168 = (bf16[32,128,128]{2,1,0:T(8,128)(2,1)S(1)}, bf16[32,32,128]{2,1,0:T(8,128)(2,1)S(1)}, bf16[16,32,128]{2,1,0:T(8,128)(2,1)S(1)}) custom-call(bf16[16,128,128]{2,1,0:T(8,128)(2,1)S(1)} %all_to_all.42.received, bf16[256,512]{1,0:T(8,128)(2,1)S(1)} %copy-done.6, f32[32,128,128]{2,1,0:T(8,128)S(1)} %get-tuple-element.19.total, ...), custom_call_target="tpu_custom_call" | custom-call | tf_op jit(solution)/shard_map/pallas_call | solution.py:283
  72.7 11.3 %all_to_all.43.received = bf16[16,32,128]{2,1,0:T(8,128)(2,1)S(1)} all-to-all(bf16[16,32,128]{2,1,0:T(8,128)(2,1)S(1)} %get-tuple-element.20), channel_id=1, replica_groups=mesh['px'=8,'py'=16] {'py'}, dimensions={0} | all-to-all | bytes 262144 | tf_op jit(solution)/shard_map/all_to_all | solution.py:294
  84.1 0.3 shard_map.169
  84.4 7.6 %all_to_all.44 = bf16[8,32,128]{2,1,0:T(8,128)(2,1)S(1)} all-to-all(bf16[8,32,128]{2,1,0:T(8,128)(2,1)S(1)} %shard_map.169), channel_id=1, replica_groups=mesh['px'=8,'py'=16] {'px'}, dimensions={0} | all-to-all | bytes 131072 | tf_op jit(solution)/shard_map/all_to_all | solution.py:294
  92.0 1.1 shard_map.170
  93.0 7.6 %all_to_all.45.received = bf16[8,32,128]{2,1,0:T(8,128)(2,1)S(1)} all-to-all(bf16[8,32,128]{2,1,0:T(8,128)(2,1)S(1)} %bitcast.27), channel_id=1, replica_groups=mesh['px'=8,'py'=16] {'px'}, dimensions={0} | all-to-all | bytes 131072 | tf_op jit(solution)/shard_map/all_to_all | solution.py:294
  100.9 12.9 %all_to_all.46.received = bf16[16,32,128]{2,1,0:T(8,128)(2,1)S(1)} all-to-all(bf16[16,32,128]{2,1,0:T(8,128)(2,1)S(1)} %shard_map.171), channel_id=1, replica_groups=mesh['px'=8,'py'=16] {'py'}, dimensions={0} | all-to-all | bytes 262144 | tf_op jit(solution)/shard_map/all_to_all | solution.py:294
  113.8 2.9 %shard_map.172 = bf16[4,8,128,128]{3,2,1,0:T(8,128)(2,1)} custom-call(bf16[16,32,128]{2,1,0:T(8,128)(2,1)S(1)} %all_to_all.46.received, bf16[256,512]{1,0:T(8,128)(2,1)S(1)} %copy-done.8, bf16[32,32,128]{2,1,0:T(8,128)(2,1)S(1)} %get-tuple-element.22.pooled, bf16[512,512]{1,0:T(8,128)(2,1)S(1)} %copy-done.4, f32[32]{0:T(128)S(1)} %copy-done.16, ...), custom_call_target="tpu_custom_call" | custom-call | tf_op jit(solution)/shard_map/pallas_call | solution.py:283
  (35 shorter events, 0.4 us)
Async XLA Ops:
  0.0 20.8 %copy-start.15 = (f32[32]{0:T(128)S(1)}, f32[32]{0:T(128)}, u32[]{:S(2)}) copy-start(f32[32]{0:T(128)} %bias.2) | copy-start | bytes 388
  0.0 1.2 %copy-start = (bf16[32,16,8,128]{3,2,1,0:T(8,128)(2,1)S(1)}, bf16[32,16,8,128]{3,2,1,0:T(8,128)(2,1)}, u32[]{:S(2)}) copy-start(bf16[32,16,8,128]{3,2,1,0:T(8,128)(2,1)} %param.17) | copy-start | bytes 3145732
  1.2 0.9 copy-start.7
  2.2 18.6 %copy-start.1 = (bf16[32,16,8,128]{3,2,1,0:T(8,128)(2,1)S(1)}, bf16[32,16,8,128]{3,2,1,0:T(8,128)(2,1)}, u32[]{:S(2)}) copy-start(bf16[32,16,8,128]{3,2,1,0:T(8,128)(2,1)} %param.17) | copy-start | bytes 3145732
  2.2 18.6 %copy-start.13 = (bf16[32,32]{1,0:T(8,128)(2,1)S(1)}, bf16[32,32]{1,0:T(8,128)(2,1)}, u32[]{:S(2)}) copy-start(bf16[32,32]{1,0:T(8,128)(2,1)} %mix_fine.1) | copy-start | bytes 6148
  2.2 18.6 %copy-start.14 = (bf16[32,32]{1,0:T(8,128)(2,1)S(1)}, bf16[32,32]{1,0:T(8,128)(2,1)}, u32[]{:S(2)}) copy-start(bf16[32,32]{1,0:T(8,128)(2,1)} %mix_coarse.1) | copy-start | bytes 6148
  7.1 17.0 %copy-start.18 = (bf16[4,32,128,1,1,1]{2,1,0,5,4,3:T(8,128)(2,1)S(1)}, bf16[4,32,128,1,1,1]{2,1,0,5,4,3:T(8,128)(2,1)}, u32[]{:S(2)}) copy-start(bf16[4,32,128,1,1,1]{2,1,0,5,4,3:T(8,128)(2,1)} %constant.30) | copy-start | bytes 98308
  7.1 20.4 %all-to-all-start = ((bf16[16,128,128]{2,1,0:T(8,128)(2,1)}), bf16[16,128,128]{2,1,0:T(8,128)(2,1)}, u32[]{:S(2)}, u32[]{:S(2)}) async-start(bf16[16,128,128]{2,1,0:T(8,128)(2,1)} %shard_map.163), calls=%async_computation | async-start | bytes 1048576 | tf_op jit(solution)/shard_map/all_to_all | solution.py:294
  16.2 7.8 %copy-start.17 = (bf16[2,32,32,32,4,2]{3,5,4,2,1,0:T(2,128)(2,1)S(1)}, bf16[2,32,32,32,4,2]{3,5,4,2,1,0:T(2,128)(2,1)}, u32[]{:S(2)}) copy-start(bf16[2,32,32,32,4,2]{3,5,4,2,1,0:T(2,128)(2,1)} %param.21) | copy-start | bytes 3145732
  20.8 6.8 %copy-start.12 = (bf16[64,128]{1,0:T(8,128)(2,1)S(1)}, bf16[64,128]{1,0:T(8,128)(2,1)}, u32[]{:S(2)}) copy-start(bf16[64,128]{1,0:T(8,128)(2,1)} %constant.18.clone.table.forward) | copy-start | bytes 49156
  20.8 18.1 %copy-start.9 = (bf16[128,128]{1,0:T(8,128)(2,1)S(1)}, bf16[128,128]{1,0:T(8,128)(2,1)}, u32[]{:S(2)}) copy-start(bf16[128,128]{1,0:T(8,128)(2,1)} %constant.19.clone.inverse.table) | copy-start | bytes 98308
  23.3 0.8 copy-start.3
  24.1 44.7 %copy-start.5 = (bf16[512,256]{1,0:T(8,128)(2,1)S(1)}, bf16[512,256]{1,0:T(8,128)(2,1)}, u32[]{:S(2)}) copy-start(bf16[512,256]{1,0:T(8,128)(2,1)} %constant.25.clone.next_table) | copy-start | bytes 786436
  25.3 58.8 %copy-start.11 = (bf16[64,64]{1,0:T(8,128)(2,1)S(1)}, bf16[64,64]{1,0:T(8,128)(2,1)}, u32[]{:S(2)}) copy-start(bf16[64,64]{1,0:T(8,128)(2,1)} %constant.20.clone.table.forward) | copy-start | bytes 24580
  25.3 66.7 %copy-start.10 = (bf16[64,128]{1,0:T(8,128)(2,1)S(1)}, bf16[64,128]{1,0:T(8,128)(2,1)}, u32[]{:S(2)}) copy-start(bf16[64,128]{1,0:T(8,128)(2,1)} %constant.21.clone.inverse.table) | copy-start | bytes 49156
  27.5 41.3 %copy-start.6 = (bf16[256,512]{1,0:T(8,128)(2,1)S(1)}, bf16[256,512]{1,0:T(8,128)(2,1)}, u32[]{:S(2)}) copy-start(bf16[256,512]{1,0:T(8,128)(2,1)} %constant.24.clone.table) | copy-start | bytes 786436
  38.9 1.2 %copy-start.2 = (bf16[2,32,2,32,128]{4,3,2,1,0:T(8,128)(2,1)S(1)}, bf16[2,32,2,32,128]{4,3,2,1,0:T(8,128)(2,1)}, u32[]{:S(2)}) copy-start(bf16[2,32,2,32,128]{4,3,2,1,0:T(8,128)(2,1)} %fusion.4.weights) | copy-start | bytes 3145732
  40.1 73.7 %copy-start.4 = (bf16[512,512]{1,0:T(8,128)(2,1)S(1)}, bf16[512,512]{1,0:T(8,128)(2,1)}, u32[]{:S(2)}) copy-start(bf16[512,512]{1,0:T(8,128)(2,1)} %copy-done.3) | copy-start | bytes 1572868
  40.1 73.7 %copy-start.8 = (bf16[256,512]{1,0:T(8,128)(2,1)S(1)}, bf16[256,512]{1,0:T(8,128)(2,1)}, u32[]{:S(2)}) copy-start(bf16[256,512]{1,0:T(8,128)(2,1)} %constant.26.clone.table) | copy-start | bytes 786436
  40.1 73.7 %copy-start.16 = (f32[32]{0:T(128)S(1)}, f32[32]{0:T(128)}, u32[]{:S(2)}) copy-start(f32[32]{0:T(128)} %bias.3) | copy-start | bytes 388

commit v3 on v2

--- a/solution.py
+++ b/solution.py
@@ -84,13 +84,15 @@
     return parts
 
 
-def spread_groups(product, send, rows):
+def spread_groups(product, send, rows, sent=None):
     def chunk(index, carry):
         at = pl.ds(pl.multiple_of(index * 16, 16), 16)
         for half in range(2):
             parts = swap_blocks([product[g, at, 128 * half : 128 * half + 128] for g in range(8)])
             for b in range(8):
                 send[8 * half + b, at, :] = parts[b].astype(BF16)
+        if sent is not None:
+            sent(index, at)
         return carry
 
     lax.fori_loop(0, rows // 16, chunk, 0)
@@ -108,18 +110,26 @@
     lax.fori_loop(0, rows // 16, chunk, 0)
 
 
-def depth_kernel(field, table_ref, send, values, table, product, arrived):
+def depth_kernel(field, table_ref, send_ref, values, table, product, send, arrived, left):
+    copies = [pltpu.make_async_copy(field.at[:, g], values.at[g], arrived.at[g]) for g in range(8)]
     table_copy = pltpu.make_async_copy(table_ref, table, arrived.at[8])
+    copies[0].start()
     table_copy.start()
-    copies = [pltpu.make_async_copy(field.at[:, g], values.at[g], arrived.at[g]) for g in range(8)]
-    for copy in copies:
+    for copy in copies[1:]:
         copy.start()
     table_copy.wait()
     for g in range(8):
         copies[g].wait()
         rows = jnp.concatenate([values[g, h] for h in range(4)], axis=1)
         product[g] = dot(rows, table[...])
-    spread_groups(product, send, 128)
+
+    def leave(index, at):
+        pltpu.make_async_copy(send.at[:, at, :], send_ref.at[:, at, :], left.at[index]).start()
+
+    spread_groups(product, send, 128, leave)
+    for index in range(8):
+        at = pl.ds(16 * index, 16)
+        pltpu.make_async_copy(send.at[:, at, :], send_ref.at[:, at, :], left.at[index]).wait()
 
 
 def columns_fine_kernel(received, table, send, lines):
@@ -143,7 +153,15 @@
     send[...] = lines[...].reshape(8, 32, 128).astype(BF16)
 
 
-def mix_kernel(received, forward, inverse, weights, send, modes, mixed):
+def mix_kernel(received, forward, inverse, weights_ref, send, modes, mixed, weights=None, arrived=None):
+    def weight_copy(g):
+        return pltpu.make_async_copy(weights_ref.at[:, :, g], weights.at[:, :, g], arrived.at[g])
+
+    if weights is None:
+        weights = weights_ref
+    else:
+        for g in range(8):
+            weight_copy(g).start()
     own = received.shape[2]
     data = received[...].astype(F32)
     data = jnp.concatenate([data[:, m].reshape(8 * own, 128) for m in range(4)], axis=1)
@@ -153,14 +171,16 @@
     modes[...] = out.T
 
     def step(g, sums):
+        if arrived is not None:
+            weight_copy(g).wait()
         sums = list(sums)
         base = g * 16
         for h in range(4):
             for k in range(2):
                 real = modes[pl.ds(base + 4 * k + h, 1), :]
                 imag = modes[pl.ds(base + 8 + 4 * k + h, 1), :]
-                w_real = weights[0, 8 * h + g, k].astype(F32)
-                w_imag = weights[1, 8 * h + g, k].astype(F32)
+                w_real = weights[0, h, g, k].astype(F32)
+                w_imag = weights[1, h, g, k].astype(F32)
                 sums[2 * k] = sums[2 * k] + (w_real * real - w_imag * imag)
                 sums[2 * k + 1] = sums[2 * k + 1] + (w_real * imag + w_imag * real)
         return tuple(sums)
@@ -214,10 +234,12 @@
 
 def pointwise_kernel(field, mix_fine, bias, mix_coarse, total, map_coarse):
     channels = channel_map(mix_fine[...])
-    for p in range(8):
-        out = dot(channels, field[:, 16 * p : 16 * p + 16, :].reshape(512, 128)).reshape(C, 16, 128)
+    for pair in range(4):
+        rows = [slice(32 * pair + 16 * e, 32 * pair + 16 * e + 16) for e in range(2)]
+        out = dot(channels, jnp.concatenate([field[:, at, :].reshape(512, 128) for at in rows], axis=1))
         for o in range(C):
-            total[o, 16 * p : 16 * p + 16, :] = out[o] + bias[o]
+            for e in range(2):
+                total[o, rows[e], :] = out[16 * o : 16 * o + 16, 128 * e : 128 * e + 128] + bias[o]
     map_coarse[...] = channel_map(mix_coarse[...])
 
 
@@ -290,6 +312,9 @@
     )(*operands)
 
 
+hold = pltpu.with_memory_space_constraint
+
+
 def exchange(x, axis):
     return lax.all_to_all(x, axis, 0, 0, tiled=True)
 
@@ -307,19 +332,24 @@
     x = call(
         depth_kernel,
         [((16, 128, 128), BF16)],
-        field.reshape(4, 8, 128, 128),
-        jnp.asarray(depth_forward(128, 1)),
+        hold(field.reshape(4, 8, 128, 128), pltpu.HBM),
+        hold(jnp.asarray(depth_forward(128, 1)), pltpu.HBM),
         specs=[HBM, HBM],
+        out_specs=[HBM],
         scratch=[
             ((8, 4, 128, 128), BF16),
             ((512, 256), BF16),
             ((8, 128, 256), F32),
+            ((16, 128, 128), BF16),
             pltpu.SemaphoreType.DMA((9,)),
+            pltpu.SemaphoreType.DMA((8,)),
         ],
     )
     x = exchange(x, "py")
     weights_fine = lay_out(spec_fine)
+    spec_coarse, weights_fine = lax.optimization_barrier((spec_coarse, weights_fine))
     weights_coarse = lay_out(spec_coarse)
+    field, weights_coarse = lax.optimization_barrier((field, weights_coarse))
     total, map_coarse = call(
         pointwise_kernel,
         [((C, 128, 128), F32), ((512, 512), BF16)],
@@ -332,10 +362,13 @@
     x, weights_fine, weights_coarse, total, map_coarse = lax.optimization_barrier(
         (x, weights_fine, weights_coarse, total, map_coarse)
     )
+    weights_fine = hold(weights_fine.reshape(2, 4, 8, 2, C, 128), pltpu.HBM)
+    weights_coarse = weights_coarse.reshape(2, 4, 8, 2, C, 128)
     x = call(columns_fine_kernel, [((8, 64, 128), BF16)], x, forward_fine, scratch=[((512, 128), F32)])
     x = exchange(x, "px").reshape(8, 4, 16, 128)
     mix_scratch = [((128, 128), F32), ((128, 128), F32)]
-    x = call(mix_kernel, [((8, 4, 16, 128), BF16)], x, forward_fine, inverse_fine, weights_fine, scratch=mix_scratch)
+    own_weights = [((2, 4, 8, 2, C, 128), BF16), pltpu.SemaphoreType.DMA((8,))]
+    x = call(mix_kernel, [((8, 4, 16, 128), BF16)], x, forward_fine, inverse_fine, weights_fine, specs=[VMEM, VMEM, VMEM, HBM], scratch=mix_scratch + own_weights)
     x = exchange(x.reshape(8, 64, 128), "px")
     x = call(back_fine_kernel, [((16, 128, 128), BF16)], x, inverse_fine, scratch=[((512, 128), F32)])
     x = exchange(x, "py")

time: 117 us -> 113 us (0.966)
  local copies, waits for them, and re-layouts: 4.26 us -> 0.08 us
    unnamed x38 -> x30, local copies, waits for them, and re-layouts: 4.26 us -> 0.08 us
  transfers between devices with their start and end apart: 1 -> 1, of which waited for: 1 -> 1; matrix products, arithmetic and copies ran while one was open for 5% -> 6% of each run, Pallas kernels for 2% -> 2%
where the time goes in v3:
time: 113 us
  blocking collectives  75.8 us (67%)
  Pallas kernels  18.3 us (16%)
  starting transfers between devices  9.13 us (8%)
  matrix products  6.44 us (6%)
  waiting for transfers between devices  2.86 us (3%)
    all_to_all x7, blocking collectives, exchange(): return lax.all_to_all(x, axis, 0, 0, tiled=True)  75.8 us
    pallas_call x10, Pallas kernels, call(): pl.pallas_call(kernel, out_shape=shapes if len(shapes) > 1 else shapes[0]...  18.3 us
    all_to_all x1, starting transfers between devices, exchange(): return lax.all_to_all(x, axis, 0, 0, tiled=True)  9.13 us
    dot_general x2, matrix products, lay_out(): jnp.einsum('riojmk,mjl->rikol', spectral, place, preferred_element_type=B...  6.44 us
    all_to_all x1, waiting for transfers between devices, exchange(): return lax.all_to_all(x, axis, 0, 0, tiled=True)  2.86 us
  transfers between devices with their start and end apart: 1, of which 1 were waited for; matrix products, arithmetic and copies ran while one was open for 6% of the time, Pallas kernels for 2%

profile of v3, /device:TPU:1, one launch (start us, length us, event | category | flops | bytes accessed | tf_op | source)
XLA Modules:
  0.0 112.8 jit_solution(9395465160152351207)
XLA Ops:
  0.0 5.5 %shard_map.163 = bf16[16,128,128]{2,1,0:T(8,128)(2,1)} custom-call(bf16[4,8,128,128]{3,2,1,0:T(8,128)(2,1)} %bitcast.24, bf16[512,256]{1,0:T(8,128)(2,1)} %constant.22.clone.table_ref), custom_call_target="tpu_custom_call" | custom-call | tf_op jit(solution)/shard_map/pallas_call | solution.py:305
  5.5 9.1 %all-to-all-start = ((bf16[16,128,128]{2,1,0:T(8,128)(2,1)}), bf16[16,128,128]{2,1,0:T(8,128)(2,1)S(1)}, u32[]{:S(2)}, u32[]{:S(2)}) async-start(bf16[16,128,128]{2,1,0:T(8,128)(2,1)} %shard_map.163), calls=%async_computation | async-start | bytes 1048576 | tf_op jit(solution)/shard_map/all_to_all | solution.py:319
  14.6 4.6 %fusion.4 = bf16[2,32,2,32,128]{4,3,2,1,0:T(8,128)(2,1)} fusion(bf16[4,32,128,1,1,1]{2,1,0,5,4,3:T(8,128)(2,1)} %constant.30, bf16[2,32,32,32,4,2]{3,5,4,2,1,0:T(2,128)(2,1)} %param.18), kind=kOutput, calls=%fused_computation.4 | convolution fusion | flops 134217728 | bytes 2129920 | tf_op jit(solution)/shard_map/riojmk,mjl->rikol/dot_general | solution.py:324
  19.2 0.0 copy-start.8
  19.2 0.0 copy-start.5
  19.2 1.9 %fusion.7 = bf16[2,32,2,32,128]{4,3,2,1,0:T(8,128)(2,1)} fusion(bf16[4,32,128,1,1,1]{2,1,0,5,4,3:T(8,128)(2,1)S(1)} %copy-done.14, bf16[2,32,32,32,4,2]{3,5,4,2,1,0:T(2,128)(2,1)S(1)} %copy-done.13), kind=kOutput, calls=%fused_computation.5 | convolution fusion | flops 134217728 | bytes 2129920 | tf_op jit(solution)/shard_map/riojmk,mjl->rikol/dot_general | solution.py:324
  21.1 0.0 copy-start.7
  21.1 1.8 %shard_map.164 = (f32[32,128,128]{2,1,0:T(8,128)S(1)}, bf16[512,512]{1,0:T(8,128)(2,1)S(1)}) custom-call(bf16[32,128,128]{2,1,0:T(8,128)(2,1)S(1)} %bitcast.25, bf16[32,32]{1,0:T(8,128)(2,1)S(1)} %copy-done.9, f32[32]{0:T(128)S(1)} %copy-done.11, bf16[32,32]{1,0:T(8,128)(2,1)S(1)} %copy-done.10), custom_call_target="tpu_custom_call" | custom-call | tf_op jit(solution)/shard_map/pallas_call | solution.py:305
  22.9 2.9 %all-to-all-done.received = bf16[16,128,128]{2,1,0:T(8,128)(2,1)S(1)} async-done(((bf16[16,128,128]{2,1,0:T(8,128)(2,1)}), bf16[16,128,128]{2,1,0:T(8,128)(2,1)S(1)}, u32[]{:S(2)}, u32[]{:S(2)}) %all-to-all-start) | async-done | bytes 524320 | tf_op jit(solution)/shard_map/all_to_all | solution.py:319
  25.8 0.4 shard_map.165
  26.2 9.9 %all_to_all.40 = bf16[8,64,128]{2,1,0:T(8,128)(2,1)S(1)} all-to-all(bf16[8,64,128]{2,1,0:T(8,128)(2,1)S(1)} %shard_map.165), channel_id=1, replica_groups=mesh['px'=8,'py'=16] {'px'}, dimensions={0} | all-to-all | bytes 262144 | tf_op jit(solution)/shard_map/all_to_all | solution.py:319
  36.1 1.8 %shard_map.166 = bf16[8,4,16,128]{3,2,1,0:T(8,128)(2,1)S(1)} custom-call(bf16[8,4,16,128]{3,2,1,0:T(8,128)(2,1)S(1)} %bitcast.27, bf16[64,128]{1,0:T(8,128)(2,1)S(1)} %copy-done.8, bf16[128,128]{1,0:T(8,128)(2,1)S(1)} %copy-done.5, bf16[2,4,8,2,32,128]{5,4,3,2,1,0:T(8,128)(2,1)} %bitcast.31), custom_call_target="tpu_custom_call" | custom-call | tf_op jit(solution)/shard_map/pallas_call | solution.py:305
  37.9 8.0 %all_to_all.41.received = bf16[8,64,128]{2,1,0:T(8,128)(2,1)S(1)} all-to-all(bf16[8,64,128]{2,1,0:T(8,128)(2,1)S(1)} %bitcast.28), channel_id=1, replica_groups=mesh['px'=8,'py'=16] {'px'}, dimensions={0} | all-to-all | bytes 262144 | tf_op jit(solution)/shard_map/all_to_all | solution.py:319
  45.9 0.4 shard_map.167
  46.3 18.6 %all_to_all.42.received = bf16[16,128,128]{2,1,0:T(8,128)(2,1)S(1)} all-to-all(bf16[16,128,128]{2,1,0:T(8,128)(2,1)S(1)} %shard_map.167), channel_id=1, replica_groups=mesh['px'=8,'py'=16] {'py'}, dimensions={0} | all-to-all | bytes 1048576 | tf_op jit(solution)/shard_map/all_to_all | solution.py:319
  64.9 3.9 %shard_map.168 = (bf16[32,128,128]{2,1,0:T(8,128)(2,1)S(1)}, bf16[32,32,128]{2,1,0:T(8,128)(2,1)S(1)}, bf16[16,32,128]{2,1,0:T(8,128)(2,1)S(1)}) custom-call(bf16[16,128,128]{2,1,0:T(8,128)(2,1)S(1)} %all_to_all.42.received, bf16[256,512]{1,0:T(8,128)(2,1)S(1)} %copy-done.3, f32[32,128,128]{2,1,0:T(8,128)S(1)} %get-tuple-element.27.total, ...), custom_call_target="tpu_custom_call" | custom-call | tf_op jit(solution)/shard_map/pallas_call | solution.py:305
  68.8 11.3 %all_to_all.43.received = bf16[16,32,128]{2,1,0:T(8,128)(2,1)S(1)} all-to-all(bf16[16,32,128]{2,1,0:T(8,128)(2,1)S(1)} %get-tuple-element.28), channel_id=1, replica_groups=mesh['px'=8,'py'=16] {'py'}, dimensions={0} | all-to-all | bytes 262144 | tf_op jit(solution)/shard_map/all_to_all | solution.py:319
  80.1 0.3 shard_map.169
  80.4 7.6 %all_to_all.44 = bf16[8,32,128]{2,1,0:T(8,128)(2,1)S(1)} all-to-all(bf16[8,32,128]{2,1,0:T(8,128)(2,1)S(1)} %shard_map.169), channel_id=1, replica_groups=mesh['px'=8,'py'=16] {'px'}, dimensions={0} | all-to-all | bytes 131072 | tf_op jit(solution)/shard_map/all_to_all | solution.py:319
  88.0 1.1 shard_map.170
  89.1 7.6 %all_to_all.45.received = bf16[8,32,128]{2,1,0:T(8,128)(2,1)S(1)} all-to-all(bf16[8,32,128]{2,1,0:T(8,128)(2,1)S(1)} %bitcast.30), channel_id=1, replica_groups=mesh['px'=8,'py'=16] {'px'}, dimensions={0} | all-to-all | bytes 131072 | tf_op jit(solution)/shard_map/all_to_all | solution.py:319
  96.7 0.3 shard_map.171
  97.0 12.9 %all_to_all.46.received = bf16[16,32,128]{2,1,0:T(8,128)(2,1)S(1)} all-to-all(bf16[16,32,128]{2,1,0:T(8,128)(2,1)S(1)} %shard_map.171), channel_id=1, replica_groups=mesh['px'=8,'py'=16] {'py'}, dimensions={0} | all-to-all | bytes 262144 | tf_op jit(solution)/shard_map/all_to_all | solution.py:319
  109.9 2.9 %shard_map.172 = bf16[4,8,128,128]{3,2,1,0:T(8,128)(2,1)} custom-call(bf16[16,32,128]{2,1,0:T(8,128)(2,1)S(1)} %all_to_all.46.received, bf16[256,512]{1,0:T(8,128)(2,1)S(1)} %copy-done.4, bf16[32,32,128]{2,1,0:T(8,128)(2,1)S(1)} %get-tuple-element.30.pooled, bf16[512,512]{1,0:T(8,128)(2,1)S(1)} %get-tuple-element.31.channels, f32[32]{0:T(128)S(1)} %copy-done.12, ...), custom_call_target="tpu_custom_call" | custom-call | tf_op jit(solution)/shard_map/pallas_call | solution.py:305
  (27 shorter events, 0.1 us)
Async XLA Ops:
  0.0 19.2 %copy-start.14 = (bf16[4,32,128,1,1,1]{2,1,0,5,4,3:T(8,128)(2,1)S(1)}, bf16[4,32,128,1,1,1]{2,1,0,5,4,3:T(8,128)(2,1)}, u32[]{:S(2)}) copy-start(bf16[4,32,128,1,1,1]{2,1,0,5,4,3:T(8,128)(2,1)} %constant.30) | copy-start | bytes 98308
  5.5 20.3 %all-to-all-start = ((bf16[16,128,128]{2,1,0:T(8,128)(2,1)}), bf16[16,128,128]{2,1,0:T(8,128)(2,1)S(1)}, u32[]{:S(2)}, u32[]{:S(2)}) async-start(bf16[16,128,128]{2,1,0:T(8,128)(2,1)} %shard_map.163), calls=%async_computation | async-start | bytes 1048576 | tf_op jit(solution)/shard_map/all_to_all | solution.py:319
  14.6 4.6 %copy-start.13 = (bf16[2,32,32,32,4,2]{3,5,4,2,1,0:T(2,128)(2,1)S(1)}, bf16[2,32,32,32,4,2]{3,5,4,2,1,0:T(2,128)(2,1)}, u32[]{:S(2)}) copy-start(bf16[2,32,32,32,4,2]{3,5,4,2,1,0:T(2,128)(2,1)} %param.21) | copy-start | bytes 3145732
  19.2 2.0 %copy-start = (bf16[32,16,8,128]{3,2,1,0:T(8,128)(2,1)S(1)}, bf16[32,16,8,128]{3,2,1,0:T(8,128)(2,1)}, u32[]{:S(2)}) copy-start(bf16[32,16,8,128]{3,2,1,0:T(8,128)(2,1)} %param.17) | copy-start | bytes 3145732
  19.2 2.0 %copy-start.9 = (bf16[32,32]{1,0:T(8,128)(2,1)S(1)}, bf16[32,32]{1,0:T(8,128)(2,1)}, u32[]{:S(2)}) copy-start(bf16[32,32]{1,0:T(8,128)(2,1)} %mix_fine.1) | copy-start | bytes 6148
  19.2 1.9 %copy-start.10 = (bf16[32,32]{1,0:T(8,128)(2,1)S(1)}, bf16[32,32]{1,0:T(8,128)(2,1)}, u32[]{:S(2)}) copy-start(bf16[32,32]{1,0:T(8,128)(2,1)} %mix_coarse.1) | copy-start | bytes 6148
  19.2 1.9 %copy-start.11 = (f32[32]{0:T(128)S(1)}, f32[32]{0:T(128)}, u32[]{:S(2)}) copy-start(f32[32]{0:T(128)} %bias.2) | copy-start | bytes 388
  19.2 6.6 %copy-start.8 = (bf16[64,128]{1,0:T(8,128)(2,1)S(1)}, bf16[64,128]{1,0:T(8,128)(2,1)}, u32[]{:S(2)}) copy-start(bf16[64,128]{1,0:T(8,128)(2,1)} %constant.18.clone.table.forward) | copy-start | bytes 49156
  19.2 16.9 %copy-start.5 = (bf16[128,128]{1,0:T(8,128)(2,1)S(1)}, bf16[128,128]{1,0:T(8,128)(2,1)}, u32[]{:S(2)}) copy-start(bf16[128,128]{1,0:T(8,128)(2,1)} %constant.19.clone.inverse.table) | copy-start | bytes 98308
  21.1 43.8 %copy-start.2 = (bf16[512,256]{1,0:T(8,128)(2,1)S(1)}, bf16[512,256]{1,0:T(8,128)(2,1)}, u32[]{:S(2)}) copy-start(bf16[512,256]{1,0:T(8,128)(2,1)} %constant.25.clone.next_table) | copy-start | bytes 786436
  21.1 59.0 %copy-start.7 = (bf16[64,64]{1,0:T(8,128)(2,1)S(1)}, bf16[64,64]{1,0:T(8,128)(2,1)}, u32[]{:S(2)}) copy-start(bf16[64,64]{1,0:T(8,128)(2,1)} %constant.20.clone.table.forward) | copy-start | bytes 24580
  22.9 65.1 %copy-start.6 = (bf16[64,128]{1,0:T(8,128)(2,1)S(1)}, bf16[64,128]{1,0:T(8,128)(2,1)}, u32[]{:S(2)}) copy-start(bf16[64,128]{1,0:T(8,128)(2,1)} %constant.21.clone.inverse.table) | copy-start | bytes 49156
  25.8 39.1 %copy-start.3 = (bf16[256,512]{1,0:T(8,128)(2,1)S(1)}, bf16[256,512]{1,0:T(8,128)(2,1)}, u32[]{:S(2)}) copy-start(bf16[256,512]{1,0:T(8,128)(2,1)} %constant.24.clone.table) | copy-start | bytes 786436
  25.8 62.2 %copy-start.1 = (bf16[2,32,2,32,128]{4,3,2,1,0:T(8,128)(2,1)S(1)}, bf16[2,32,2,32,128]{4,3,2,1,0:T(8,128)(2,1)}, u32[]{:S(2)}) copy-start(bf16[2,32,2,32,128]{4,3,2,1,0:T(8,128)(2,1)} %fusion.7) | copy-start | bytes 3145732
  36.1 73.8 %copy-start.4 = (bf16[256,512]{1,0:T(8,128)(2,1)S(1)}, bf16[256,512]{1,0:T(8,128)(2,1)}, u32[]{:S(2)}) copy-start(bf16[256,512]{1,0:T(8,128)(2,1)} %constant.26.clone.table) | copy-start | bytes 786436
  36.1 73.8 %copy-start.12 = (f32[32]{0:T(128)S(1)}, f32[32]{0:T(128)}, u32[]{:S(2)}) copy-start(f32[32]{0:T(128)} %bias.3) | copy-start | bytes 388

commit v4 on v3

--- a/solution.py
+++ b/solution.py
@@ -95,7 +95,7 @@
             sent(index, at)
         return carry
 
-    lax.fori_loop(0, rows // 16, chunk, 0)
+    lax.fori_loop(0, rows // 16, chunk, 0, unroll=min(2, rows // 16))
 
 
 def collect_groups(received, spread, rows):
@@ -107,7 +107,7 @@
                 spread[g, at, 128 * half : 128 * half + 128] = parts[g].astype(BF16)
         return carry
 
-    lax.fori_loop(0, rows // 16, chunk, 0)
+    lax.fori_loop(0, rows // 16, chunk, 0, unroll=min(2, rows // 16))
 
 
 def depth_kernel(field, table_ref, send_ref, values, table, product, send, arrived, left):
@@ -118,10 +118,17 @@
     for copy in copies[1:]:
         copy.start()
     table_copy.wait()
-    for g in range(8):
-        copies[g].wait()
-        rows = jnp.concatenate([values[g, h] for h in range(4)], axis=1)
-        product[g] = dot(rows, table[...])
+
+    def group(pair, carry):
+        for e in range(2):
+            g = 2 * pair + e
+            pltpu.make_async_copy(field.at[:, g], values.at[g], arrived.at[g]).wait()
+        for e in range(2):
+            rows = jnp.concatenate([values[2 * pair + e, h] for h in range(4)], axis=1)
+            product[2 * pair + e] = dot(rows, table[...])
+        return carry
+
+    lax.fori_loop(0, 4, group, 0)
 
     def leave(index, at):
         pltpu.make_async_copy(send.at[:, at, :], send_ref.at[:, at, :], left.at[index]).start()

time: 113 us -> 110 us (0.973)
  Pallas kernels: 18.3 us -> 15 us
    pallas_call x10, Pallas kernels: 18.3 us -> 15 us  [call(): pl.pallas_call(kernel, out_shape=shapes if len(shapes) > 1 else shapes[0]...]
where the time goes in v4:
time: 110 us; the launch traced here: 109 us
  blocking collectives  75.8 us (69%)
  Pallas kernels  15 us (14%)
  starting transfers between devices  9.13 us (8%)
  matrix products  6.43 us (6%)
  waiting for transfers between devices  2.86 us (3%)
    all_to_all x7, blocking collectives, exchange(): return lax.all_to_all(x, axis, 0, 0, tiled=True)  75.8 us
    pallas_call x10, Pallas kernels, call(): pl.pallas_call(kernel, out_shape=shapes if len(shapes) > 1 else shapes[0]...  15 us
    all_to_all x1, starting transfers between devices, exchange(): return lax.all_to_all(x, axis, 0, 0, tiled=True)  9.13 us
    dot_general x2, matrix products, lay_out(): jnp.einsum('riojmk,mjl->rikol', spectral, place, preferred_element_type=B...  6.43 us
    all_to_all x1, waiting for transfers between devices, exchange(): return lax.all_to_all(x, axis, 0, 0, tiled=True)  2.86 us
  transfers between devices with their start and end apart: 1, of which 1 were waited for; matrix products, arithmetic and copies ran while one was open for 6% of the time, Pallas kernels for 2%

profile of v4, /device:TPU:1, one launch (start us, length us, event | category | flops | bytes accessed | tf_op | source)
XLA Modules:
  0.0 109.5 jit_solution(6708230824001107844)
XLA Ops:
  0.0 3.8 %shard_map.163 = bf16[16,128,128]{2,1,0:T(8,128)(2,1)} custom-call(bf16[4,8,128,128]{3,2,1,0:T(8,128)(2,1)} %bitcast.24, bf16[512,256]{1,0:T(8,128)(2,1)} %constant.22.clone.table_ref), custom_call_target="tpu_custom_call" | custom-call | tf_op jit(solution)/shard_map/pallas_call | solution.py:312
  3.8 9.1 %all-to-all-start = ((bf16[16,128,128]{2,1,0:T(8,128)(2,1)}), bf16[16,128,128]{2,1,0:T(8,128)(2,1)S(1)}, u32[]{:S(2)}, u32[]{:S(2)}) async-start(bf16[16,128,128]{2,1,0:T(8,128)(2,1)} %shard_map.163), calls=%async_computation | async-start | bytes 1048576 | tf_op jit(solution)/shard_map/all_to_all | solution.py:326
  13.0 4.6 %fusion.4 = bf16[2,32,2,32,128]{4,3,2,1,0:T(8,128)(2,1)} fusion(bf16[4,32,128,1,1,1]{2,1,0,5,4,3:T(8,128)(2,1)} %constant.30, bf16[2,32,32,32,4,2]{3,5,4,2,1,0:T(2,128)(2,1)} %param.18), kind=kOutput, calls=%fused_computation.4 | convolution fusion | flops 134217728 | bytes 2129920 | tf_op jit(solution)/shard_map/riojmk,mjl->rikol/dot_general | solution.py:331
  17.6 0.0 copy-start.8
  17.6 0.0 copy-start.5
  17.6 1.9 %fusion.7 = bf16[2,32,2,32,128]{4,3,2,1,0:T(8,128)(2,1)} fusion(bf16[4,32,128,1,1,1]{2,1,0,5,4,3:T(8,128)(2,1)S(1)} %copy-done.14, bf16[2,32,32,32,4,2]{3,5,4,2,1,0:T(2,128)(2,1)S(1)} %copy-done.13), kind=kOutput, calls=%fused_computation.5 | convolution fusion | flops 134217728 | bytes 2129920 | tf_op jit(solution)/shard_map/riojmk,mjl->rikol/dot_general | solution.py:331
  19.5 0.0 copy-start.7
  19.5 1.8 %shard_map.164 = (f32[32,128,128]{2,1,0:T(8,128)S(1)}, bf16[512,512]{1,0:T(8,128)(2,1)S(1)}) custom-call(bf16[32,128,128]{2,1,0:T(8,128)(2,1)S(1)} %bitcast.25, bf16[32,32]{1,0:T(8,128)(2,1)S(1)} %copy-done.9, f32[32]{0:T(128)S(1)} %copy-done.11, bf16[32,32]{1,0:T(8,128)(2,1)S(1)} %copy-done.10), custom_call_target="tpu_custom_call" | custom-call | tf_op jit(solution)/shard_map/pallas_call | solution.py:312
  21.3 2.9 %all-to-all-done.received = bf16[16,128,128]{2,1,0:T(8,128)(2,1)S(1)} async-done(((bf16[16,128,128]{2,1,0:T(8,128)(2,1)}), bf16[16,128,128]{2,1,0:T(8,128)(2,1)S(1)}, u32[]{:S(2)}, u32[]{:S(2)}) %all-to-all-start) | async-done | bytes 524320 | tf_op jit(solution)/shard_map/all_to_all | solution.py:326
  24.2 0.4 shard_map.165
  24.6 9.9 %all_to_all.40 = bf16[8,64,128]{2,1,0:T(8,128)(2,1)S(1)} all-to-all(bf16[8,64,128]{2,1,0:T(8,128)(2,1)S(1)} %shard_map.165), channel_id=1, replica_groups=mesh['px'=8,'py'=16] {'px'}, dimensions={0} | all-to-all | bytes 262144 | tf_op jit(solution)/shard_map/all_to_all | solution.py:326
  34.4 1.8 %shard_map.166 = bf16[8,4,16,128]{3,2,1,0:T(8,128)(2,1)S(1)} custom-call(bf16[8,4,16,128]{3,2,1,0:T(8,128)(2,1)S(1)} %bitcast.27, bf16[64,128]{1,0:T(8,128)(2,1)S(1)} %copy-done.8, bf16[128,128]{1,0:T(8,128)(2,1)S(1)} %copy-done.5, bf16[2,4,8,2,32,128]{5,4,3,2,1,0:T(8,128)(2,1)} %bitcast.31), custom_call_target="tpu_custom_call" | custom-call | tf_op jit(solution)/shard_map/pallas_call | solution.py:312
  36.3 8.0 %all_to_all.41.received = bf16[8,64,128]{2,1,0:T(8,128)(2,1)S(1)} all-to-all(bf16[8,64,128]{2,1,0:T(8,128)(2,1)S(1)} %bitcast.28), channel_id=1, replica_groups=mesh['px'=8,'py'=16] {'px'}, dimensions={0} | all-to-all | bytes 262144 | tf_op jit(solution)/shard_map/all_to_all | solution.py:326
  44.3 0.4 shard_map.167
  44.7 18.6 %all_to_all.42.received = bf16[16,128,128]{2,1,0:T(8,128)(2,1)S(1)} all-to-all(bf16[16,128,128]{2,1,0:T(8,128)(2,1)S(1)} %shard_map.167), channel_id=1, replica_groups=mesh['px'=8,'py'=16] {'py'}, dimensions={0} | all-to-all | bytes 1048576 | tf_op jit(solution)/shard_map/all_to_all | solution.py:326
  63.2 2.8 %shard_map.168 = (bf16[32,128,128]{2,1,0:T(8,128)(2,1)S(1)}, bf16[32,32,128]{2,1,0:T(8,128)(2,1)S(1)}, bf16[16,32,128]{2,1,0:T(8,128)(2,1)S(1)}) custom-call(bf16[16,128,128]{2,1,0:T(8,128)(2,1)S(1)} %all_to_all.42.received, bf16[256,512]{1,0:T(8,128)(2,1)S(1)} %copy-done.3, f32[32,128,128]{2,1,0:T(8,128)S(1)} %get-tuple-element.27.total, ...), custom_call_target="tpu_custom_call" | custom-call | tf_op jit(solution)/shard_map/pallas_call | solution.py:312
  66.1 11.3 %all_to_all.43.received = bf16[16,32,128]{2,1,0:T(8,128)(2,1)S(1)} all-to-all(bf16[16,32,128]{2,1,0:T(8,128)(2,1)S(1)} %get-tuple-element.28), channel_id=1, replica_groups=mesh['px'=8,'py'=16] {'py'}, dimensions={0} | all-to-all | bytes 262144 | tf_op jit(solution)/shard_map/all_to_all | solution.py:326
  77.4 0.3 shard_map.169
  77.7 7.6 %all_to_all.44 = bf16[8,32,128]{2,1,0:T(8,128)(2,1)S(1)} all-to-all(bf16[8,32,128]{2,1,0:T(8,128)(2,1)S(1)} %shard_map.169), channel_id=1, replica_groups=mesh['px'=8,'py'=16] {'px'}, dimensions={0} | all-to-all | bytes 131072 | tf_op jit(solution)/shard_map/all_to_all | solution.py:326
  85.3 1.1 shard_map.170
  86.4 7.6 %all_to_all.45.received = bf16[8,32,128]{2,1,0:T(8,128)(2,1)S(1)} all-to-all(bf16[8,32,128]{2,1,0:T(8,128)(2,1)S(1)} %bitcast.30), channel_id=1, replica_groups=mesh['px'=8,'py'=16] {'px'}, dimensions={0} | all-to-all | bytes 131072 | tf_op jit(solution)/shard_map/all_to_all | solution.py:326
  93.9 0.3 shard_map.171
  94.3 12.9 %all_to_all.46.received = bf16[16,32,128]{2,1,0:T(8,128)(2,1)S(1)} all-to-all(bf16[16,32,128]{2,1,0:T(8,128)(2,1)S(1)} %shard_map.171), channel_id=1, replica_groups=mesh['px'=8,'py'=16] {'py'}, dimensions={0} | all-to-all | bytes 262144 | tf_op jit(solution)/shard_map/all_to_all | solution.py:326
  107.2 2.3 %shard_map.172 = bf16[4,8,128,128]{3,2,1,0:T(8,128)(2,1)} custom-call(bf16[16,32,128]{2,1,0:T(8,128)(2,1)S(1)} %all_to_all.46.received, bf16[256,512]{1,0:T(8,128)(2,1)S(1)} %copy-done.4, bf16[32,32,128]{2,1,0:T(8,128)(2,1)S(1)} %get-tuple-element.30.pooled, bf16[512,512]{1,0:T(8,128)(2,1)S(1)} %get-tuple-element.31.channels, f32[32]{0:T(128)S(1)} %copy-done.12, ...), custom_call_target="tpu_custom_call" | custom-call | tf_op jit(solution)/shard_map/pallas_call | solution.py:312
  (27 shorter events, 0.1 us)
Async XLA Ops:
  0.0 17.5 %copy-start.14 = (bf16[4,32,128,1,1,1]{2,1,0,5,4,3:T(8,128)(2,1)S(1)}, bf16[4,32,128,1,1,1]{2,1,0,5,4,3:T(8,128)(2,1)}, u32[]{:S(2)}) copy-start(bf16[4,32,128,1,1,1]{2,1,0,5,4,3:T(8,128)(2,1)} %constant.30) | copy-start | bytes 98308
  3.8 20.3 %all-to-all-start = ((bf16[16,128,128]{2,1,0:T(8,128)(2,1)}), bf16[16,128,128]{2,1,0:T(8,128)(2,1)S(1)}, u32[]{:S(2)}, u32[]{:S(2)}) async-start(bf16[16,128,128]{2,1,0:T(8,128)(2,1)} %shard_map.163), calls=%async_computation | async-start | bytes 1048576 | tf_op jit(solution)/shard_map/all_to_all | solution.py:326
  13.0 4.6 %copy-start.13 = (bf16[2,32,32,32,4,2]{3,5,4,2,1,0:T(2,128)(2,1)S(1)}, bf16[2,32,32,32,4,2]{3,5,4,2,1,0:T(2,128)(2,1)}, u32[]{:S(2)}) copy-start(bf16[2,32,32,32,4,2]{3,5,4,2,1,0:T(2,128)(2,1)} %param.21) | copy-start | bytes 3145732
  17.5 2.0 %copy-start = (bf16[32,16,8,128]{3,2,1,0:T(8,128)(2,1)S(1)}, bf16[32,16,8,128]{3,2,1,0:T(8,128)(2,1)}, u32[]{:S(2)}) copy-start(bf16[32,16,8,128]{3,2,1,0:T(8,128)(2,1)} %param.17) | copy-start | bytes 3145732
  17.5 2.0 %copy-start.9 = (bf16[32,32]{1,0:T(8,128)(2,1)S(1)}, bf16[32,32]{1,0:T(8,128)(2,1)}, u32[]{:S(2)}) copy-start(bf16[32,32]{1,0:T(8,128)(2,1)} %mix_fine.1) | copy-start | bytes 6148
  17.5 1.9 %copy-start.10 = (bf16[32,32]{1,0:T(8,128)(2,1)S(1)}, bf16[32,32]{1,0:T(8,128)(2,1)}, u32[]{:S(2)}) copy-start(bf16[32,32]{1,0:T(8,128)(2,1)} %mix_coarse.1) | copy-start | bytes 6148
  17.6 1.9 %copy-start.11 = (f32[32]{0:T(128)S(1)}, f32[32]{0:T(128)}, u32[]{:S(2)}) copy-start(f32[32]{0:T(128)} %bias.2) | copy-start | bytes 388
  17.6 6.6 %copy-start.8 = (bf16[64,128]{1,0:T(8,128)(2,1)S(1)}, bf16[64,128]{1,0:T(8,128)(2,1)}, u32[]{:S(2)}) copy-start(bf16[64,128]{1,0:T(8,128)(2,1)} %constant.18.clone.table.forward) | copy-start | bytes 49156
  17.6 16.9 %copy-start.5 = (bf16[128,128]{1,0:T(8,128)(2,1)S(1)}, bf16[128,128]{1,0:T(8,128)(2,1)}, u32[]{:S(2)}) copy-start(bf16[128,128]{1,0:T(8,128)(2,1)} %constant.19.clone.inverse.table) | copy-start | bytes 98308
  19.5 43.8 %copy-start.2 = (bf16[512,256]{1,0:T(8,128)(2,1)S(1)}, bf16[512,256]{1,0:T(8,128)(2,1)}, u32[]{:S(2)}) copy-start(bf16[512,256]{1,0:T(8,128)(2,1)} %constant.25.clone.next_table) | copy-start | bytes 786436
  19.5 57.9 %copy-start.7 = (bf16[64,64]{1,0:T(8,128)(2,1)S(1)}, bf16[64,64]{1,0:T(8,128)(2,1)}, u32[]{:S(2)}) copy-start(bf16[64,64]{1,0:T(8,128)(2,1)} %constant.20.clone.table.forward) | copy-start | bytes 24580
  21.3 64.0 %copy-start.6 = (bf16[64,128]{1,0:T(8,128)(2,1)S(1)}, bf16[64,128]{1,0:T(8,128)(2,1)}, u32[]{:S(2)}) copy-start(bf16[64,128]{1,0:T(8,128)(2,1)} %constant.21.clone.inverse.table) | copy-start | bytes 49156
  24.2 39.1 %copy-start.3 = (bf16[256,512]{1,0:T(8,128)(2,1)S(1)}, bf16[256,512]{1,0:T(8,128)(2,1)}, u32[]{:S(2)}) copy-start(bf16[256,512]{1,0:T(8,128)(2,1)} %constant.24.clone.table) | copy-start | bytes 786436
  24.2 61.1 %copy-start.1 = (bf16[2,32,2,32,128]{4,3,2,1,0:T(8,128)(2,1)S(1)}, bf16[2,32,2,32,128]{4,3,2,1,0:T(8,128)(2,1)}, u32[]{:S(2)}) copy-start(bf16[2,32,2,32,128]{4,3,2,1,0:T(8,128)(2,1)} %fusion.7) | copy-start | bytes 3145732
  34.4 72.7 %copy-start.4 = (bf16[256,512]{1,0:T(8,128)(2,1)S(1)}, bf16[256,512]{1,0:T(8,128)(2,1)}, u32[]{:S(2)}) copy-start(bf16[256,512]{1,0:T(8,128)(2,1)} %constant.26.clone.table) | copy-start | bytes 786436
  34.4 72.7 %copy-start.12 = (f32[32]{0:T(128)S(1)}, f32[32]{0:T(128)}, u32[]{:S(2)}) copy-start(f32[32]{0:T(128)} %bias.3) | copy-start | bytes 388

commit v5 on v4

--- a/solution.py
+++ b/solution.py
@@ -139,7 +139,8 @@
         pltpu.make_async_copy(send.at[:, at, :], send_ref.at[:, at, :], left.at[index]).wait()
 
 
-def columns_fine_kernel(received, table, send, lines):
+def columns_fine_kernel(received, table, later, send, lines):
+    del later
     for pair in range(8):
         block = received[:, 16 * pair : 16 * pair + 16, :].astype(F32).reshape(16, 2, 8, 128)
         data = jnp.concatenate([block[:, e].reshape(128, 128) for e in range(2)], axis=1)
@@ -246,7 +247,8 @@
         out = dot(channels, jnp.concatenate([field[:, at, :].reshape(512, 128) for at in rows], axis=1))
         for o in range(C):
             for e in range(2):
-                total[o, rows[e], :] = out[16 * o : 16 * o + 16, 128 * e : 128 * e + 128] + bias[o]
+                block = out[16 * o : 16 * o + 16, 128 * e : 128 * e + 128] + bias[o]
+                total[o, rows[e], :] = block.astype(BF16)
     map_coarse[...] = channel_map(mix_coarse[...])
 
 
@@ -260,10 +262,11 @@
     collect_groups(received, spread, 128)
     even = (lanes_of((64, 128)) & 1) == 0
     for g in range(8):
-        out = dot(spread[g], table[...])
         for h in range(4):
+            if h % 2 == 0:
+                out = dot(spread[g], table[:, 128 * h : 128 * h + 256])
             o = 8 * h + g
-            value = gelu(out[:, 128 * h : 128 * h + 128] + total[o]).astype(BF16)
+            value = gelu(out[:, 128 * (h % 2) : 128 * (h % 2) + 128] + total[o].astype(F32)).astype(BF16)
             upper[o] = value
             value = value.astype(F32).reshape(8, 2, 8, 128)
             value = (value[:, 0] + value[:, 1]).reshape(64, 128)
@@ -359,7 +362,7 @@
     field, weights_coarse = lax.optimization_barrier((field, weights_coarse))
     total, map_coarse = call(
         pointwise_kernel,
-        [((C, 128, 128), F32), ((512, 512), BF16)],
+        [((C, 128, 128), BF16), ((512, 512), BF16)],
         field,
         mix_fine,
         bias_fine,
@@ -369,13 +372,13 @@
     x, weights_fine, weights_coarse, total, map_coarse = lax.optimization_barrier(
         (x, weights_fine, weights_coarse, total, map_coarse)
     )
-    weights_fine = hold(weights_fine.reshape(2, 4, 8, 2, C, 128), pltpu.HBM)
+    weights_fine = weights_fine.reshape(2, 4, 8, 2, C, 128)
     weights_coarse = weights_coarse.reshape(2, 4, 8, 2, C, 128)
-    x = call(columns_fine_kernel, [((8, 64, 128), BF16)], x, forward_fine, scratch=[((512, 128), F32)])
+    x = call(columns_fine_kernel, [((8, 64, 128), BF16)], x, forward_fine, weights_fine, scratch=[((512, 128), F32)])
     x = exchange(x, "px").reshape(8, 4, 16, 128)
     mix_scratch = [((128, 128), F32), ((128, 128), F32)]
     own_weights = [((2, 4, 8, 2, C, 128), BF16), pltpu.SemaphoreType.DMA((8,))]
-    x = call(mix_kernel, [((8, 4, 16, 128), BF16)], x, forward_fine, inverse_fine, weights_fine, specs=[VMEM, VMEM, VMEM, HBM], scratch=mix_scratch + own_weights)
+    x = call(mix_kernel, [((8, 4, 16, 128), BF16)], x, forward_fine, inverse_fine, weights_fine, scratch=mix_scratch)
     x = exchange(x.reshape(8, 64, 128), "px")
     x = call(back_fine_kernel, [((16, 128, 128), BF16)], x, inverse_fine, scratch=[((512, 128), F32)])
     x = exchange(x, "py")

time: 110 us -> 109 us (level)
  matrix products: 6.43 us -> 4.46 us
  local copies, waits for them, and re-layouts: 0.08 us -> 1.29 us
    dot_general x2, matrix products: 6.43 us -> 4.46 us  [lay_out(): jnp.einsum('riojmk,mjl->rikol', spectral, place, preferred_element_type=B...]
    unnamed x30 -> x32, local copies, waits for them, and re-layouts: 0.08 us -> 1.29 us
  transfers between devices with their start and end apart: 1 -> 1, of which waited for: 1 -> 1; matrix products, arithmetic and copies ran while one was open for 6% -> 4% of each run, Pallas kernels for 2% -> 2%
where the time goes in v5:
time: 109 us; the launch traced here: 108 us
  blocking collectives  75.5 us (69%)
  Pallas kernels  14.3 us (13%)
  starting transfers between devices  9.13 us (8%)
  matrix products  4.46 us (4%)
  waiting for transfers between devices  3.59 us (3%)
  local copies, waits for them, and re-layouts  1.29 us (1%)
    all_to_all x7, blocking collectives, exchange(): return lax.all_to_all(x, axis, 0, 0, tiled=True)  75.5 us
    pallas_call x10, Pallas kernels, call(): pl.pallas_call(kernel, out_shape=shapes if len(shapes) > 1 else shapes[0]...  14.3 us
    all_to_all x1, starting transfers between devices, exchange(): return lax.all_to_all(x, axis, 0, 0, tiled=True)  9.13 us
    dot_general x2, matrix products, lay_out(): jnp.einsum('riojmk,mjl->rikol', spectral, place, preferred_element_type=B...  4.46 us
    all_to_all x1, waiting for transfers between devices, exchange(): return lax.all_to_all(x, axis, 0, 0, tiled=True)  3.59 us
  transfers between devices with their start and end apart: 1, of which 1 were waited for; matrix products, arithmetic and copies ran while one was open for 4% of the time, Pallas kernels for 2%

profile of v5, /device:TPU:1, one launch (start us, length us, event | category | flops | bytes accessed | tf_op | source)
XLA Modules:
  0.0 108.5 jit_solution(7943463745976380422)
XLA Ops:
  0.0 3.8 %shard_map.163 = bf16[16,128,128]{2,1,0:T(8,128)(2,1)} custom-call(bf16[4,8,128,128]{3,2,1,0:T(8,128)(2,1)} %bitcast.24, bf16[512,256]{1,0:T(8,128)(2,1)} %constant.22.clone.table_ref), custom_call_target="tpu_custom_call" | custom-call | tf_op jit(solution)/shard_map/pallas_call | solution.py:315
  3.8 9.1 %all-to-all-start = ((bf16[16,128,128]{2,1,0:T(8,128)(2,1)}), bf16[16,128,128]{2,1,0:T(8,128)(2,1)S(1)}, u32[]{:S(2)}, u32[]{:S(2)}) async-start(bf16[16,128,128]{2,1,0:T(8,128)(2,1)} %shard_map.163), calls=%async_computation | async-start | bytes 1048576 | tf_op jit(solution)/shard_map/all_to_all | solution.py:329
  12.9 3.6 %fusion.4 = bf16[2,32,2,32,128]{4,3,2,1,0:T(8,128)(2,1)S(1)} fusion(bf16[4,32,128,1,1,1]{2,1,0,5,4,3:T(8,128)(2,1)} %constant.30, bf16[2,32,32,32,4,2]{3,5,4,2,1,0:T(2,128)(2,1)} %param.18), kind=kOutput, calls=%fused_computation.4 | convolution fusion | flops 134217728 | bytes 2129920 | tf_op jit(solution)/shard_map/riojmk,mjl->rikol/dot_general | solution.py:334
  16.6 0.0 copy-start.7
  16.6 0.9 fusion.7
  17.5 0.2 copy-done
  17.8 1.8 %shard_map.164 = (bf16[32,128,128]{2,1,0:T(8,128)(2,1)S(1)}, bf16[512,512]{1,0:T(8,128)(2,1)S(1)}) custom-call(bf16[32,128,128]{2,1,0:T(8,128)(2,1)S(1)} %bitcast.25, bf16[32,32]{1,0:T(8,128)(2,1)S(1)} %copy-done.10, f32[32]{0:T(128)S(1)} %copy-done.12, bf16[32,32]{1,0:T(8,128)(2,1)S(1)} %copy-done.11), custom_call_target="tpu_custom_call" | custom-call | tf_op jit(solution)/shard_map/pallas_call | solution.py:315
  19.6 1.0 copy-done.1
  20.5 3.6 %all-to-all-done.received = bf16[16,128,128]{2,1,0:T(8,128)(2,1)S(1)} async-done(((bf16[16,128,128]{2,1,0:T(8,128)(2,1)}), bf16[16,128,128]{2,1,0:T(8,128)(2,1)S(1)}, u32[]{:S(2)}, u32[]{:S(2)}) %all-to-all-start) | async-done | bytes 524320 | tf_op jit(solution)/shard_map/all_to_all | solution.py:329
  24.1 0.4 shard_map.165
  24.6 10.0 %all_to_all.40 = bf16[8,64,128]{2,1,0:T(8,128)(2,1)S(1)} all-to-all(bf16[8,64,128]{2,1,0:T(8,128)(2,1)S(1)} %shard_map.165), channel_id=1, replica_groups=mesh['px'=8,'py'=16] {'px'}, dimensions={0} | all-to-all | bytes 262144 | tf_op jit(solution)/shard_map/all_to_all | solution.py:329
  34.6 1.1 shard_map.166
  35.6 8.0 %all_to_all.41.received = bf16[8,64,128]{2,1,0:T(8,128)(2,1)S(1)} all-to-all(bf16[8,64,128]{2,1,0:T(8,128)(2,1)S(1)} %bitcast.30), channel_id=1, replica_groups=mesh['px'=8,'py'=16] {'px'}, dimensions={0} | all-to-all | bytes 262144 | tf_op jit(solution)/shard_map/all_to_all | solution.py:329
  43.6 0.4 shard_map.167
  44.0 17.8 %all_to_all.42.received = bf16[16,128,128]{2,1,0:T(8,128)(2,1)S(1)} all-to-all(bf16[16,128,128]{2,1,0:T(8,128)(2,1)S(1)} %shard_map.167), channel_id=1, replica_groups=mesh['px'=8,'py'=16] {'py'}, dimensions={0} | all-to-all | bytes 1048576 | tf_op jit(solution)/shard_map/all_to_all | solution.py:329
  61.9 2.9 %shard_map.168 = (bf16[32,128,128]{2,1,0:T(8,128)(2,1)S(1)}, bf16[32,32,128]{2,1,0:T(8,128)(2,1)S(1)}, bf16[16,32,128]{2,1,0:T(8,128)(2,1)S(1)}) custom-call(bf16[16,128,128]{2,1,0:T(8,128)(2,1)S(1)} %all_to_all.42.received, bf16[256,512]{1,0:T(8,128)(2,1)S(1)} %copy-done.5, bf16[32,128,128]{2,1,0:T(8,128)(2,1)S(1)} %copy-done.2, bf16[512,256]{1,0:T(8,128)(2,1)S(1)} %copy-done.4), custom_call_target="tpu_custom_call" | custom-call | tf_op jit(solution)/shard_map/pallas_call | solution.py:315
  64.8 11.3 %all_to_all.43.received = bf16[16,32,128]{2,1,0:T(8,128)(2,1)S(1)} all-to-all(bf16[16,32,128]{2,1,0:T(8,128)(2,1)S(1)} %get-tuple-element.28), channel_id=1, replica_groups=mesh['px'=8,'py'=16] {'py'}, dimensions={0} | all-to-all | bytes 262144 | tf_op jit(solution)/shard_map/all_to_all | solution.py:329
  76.1 0.3 shard_map.169
  76.4 7.6 %all_to_all.44 = bf16[8,32,128]{2,1,0:T(8,128)(2,1)S(1)} all-to-all(bf16[8,32,128]{2,1,0:T(8,128)(2,1)S(1)} %shard_map.169), channel_id=1, replica_groups=mesh['px'=8,'py'=16] {'px'}, dimensions={0} | all-to-all | bytes 131072 | tf_op jit(solution)/shard_map/all_to_all | solution.py:329
  84.0 1.1 shard_map.170
  85.1 7.6 %all_to_all.45.received = bf16[8,32,128]{2,1,0:T(8,128)(2,1)S(1)} all-to-all(bf16[8,32,128]{2,1,0:T(8,128)(2,1)S(1)} %bitcast.32), channel_id=1, replica_groups=mesh['px'=8,'py'=16] {'px'}, dimensions={0} | all-to-all | bytes 131072 | tf_op jit(solution)/shard_map/all_to_all | solution.py:329
  92.6 0.3 shard_map.171
  92.9 13.2 %all_to_all.46.received = bf16[16,32,128]{2,1,0:T(8,128)(2,1)S(1)} all-to-all(bf16[16,32,128]{2,1,0:T(8,128)(2,1)S(1)} %shard_map.171), channel_id=1, replica_groups=mesh['px'=8,'py'=16] {'py'}, dimensions={0} | all-to-all | bytes 262144 | tf_op jit(solution)/shard_map/all_to_all | solution.py:329
  106.2 2.3 %shard_map.172 = bf16[4,8,128,128]{3,2,1,0:T(8,128)(2,1)} custom-call(bf16[16,32,128]{2,1,0:T(8,128)(2,1)S(1)} %all_to_all.46.received, bf16[256,512]{1,0:T(8,128)(2,1)S(1)} %copy-done.3, bf16[32,32,128]{2,1,0:T(8,128)(2,1)S(1)} %get-tuple-element.30.pooled, bf16[512,512]{1,0:T(8,128)(2,1)S(1)} %get-tuple-element.31.channels, f32[32]{0:T(128)S(1)} %copy-done.13, ...), custom_call_target="tpu_custom_call" | custom-call | tf_op jit(solution)/shard_map/pallas_call | solution.py:315
  (29 shorter events, 0.1 us)
Async XLA Ops:
  0.0 16.5 %copy-start.15 = (bf16[4,32,128,1,1,1]{2,1,0,5,4,3:T(8,128)(2,1)S(1)}, bf16[4,32,128,1,1,1]{2,1,0,5,4,3:T(8,128)(2,1)}, u32[]{:S(2)}) copy-start(bf16[4,32,128,1,1,1]{2,1,0,5,4,3:T(8,128)(2,1)} %constant.30) | copy-start | bytes 98308
  3.8 20.3 %all-to-all-start = ((bf16[16,128,128]{2,1,0:T(8,128)(2,1)}), bf16[16,128,128]{2,1,0:T(8,128)(2,1)S(1)}, u32[]{:S(2)}, u32[]{:S(2)}) async-start(bf16[16,128,128]{2,1,0:T(8,128)(2,1)} %shard_map.163), calls=%async_computation | async-start | bytes 1048576 | tf_op jit(solution)/shard_map/all_to_all | solution.py:329
  12.9 3.6 %copy-start.14 = (bf16[2,32,32,32,4,2]{3,5,4,2,1,0:T(2,128)(2,1)S(1)}, bf16[2,32,32,32,4,2]{3,5,4,2,1,0:T(2,128)(2,1)}, u32[]{:S(2)}) copy-start(bf16[2,32,32,32,4,2]{3,5,4,2,1,0:T(2,128)(2,1)} %param.21) | copy-start | bytes 3145732
  16.5 1.2 %copy-start = (bf16[32,16,8,128]{3,2,1,0:T(8,128)(2,1)S(1)}, bf16[32,16,8,128]{3,2,1,0:T(8,128)(2,1)}, u32[]{:S(2)}) copy-start(bf16[32,16,8,128]{3,2,1,0:T(8,128)(2,1)} %param.17) | copy-start | bytes 3145732
  16.6 1.2 %copy-start.10 = (bf16[32,32]{1,0:T(8,128)(2,1)S(1)}, bf16[32,32]{1,0:T(8,128)(2,1)}, u32[]{:S(2)}) copy-start(bf16[32,32]{1,0:T(8,128)(2,1)} %mix_fine.1) | copy-start | bytes 6148
  16.6 1.2 %copy-start.11 = (bf16[32,32]{1,0:T(8,128)(2,1)S(1)}, bf16[32,32]{1,0:T(8,128)(2,1)}, u32[]{:S(2)}) copy-start(bf16[32,32]{1,0:T(8,128)(2,1)} %mix_coarse.1) | copy-start | bytes 6148
  16.6 1.2 %copy-start.12 = (f32[32]{0:T(128)S(1)}, f32[32]{0:T(128)}, u32[]{:S(2)}) copy-start(f32[32]{0:T(128)} %bias.2) | copy-start | bytes 388
  16.6 7.6 %copy-start.7 = (bf16[64,128]{1,0:T(8,128)(2,1)S(1)}, bf16[64,128]{1,0:T(8,128)(2,1)}, u32[]{:S(2)}) copy-start(bf16[64,128]{1,0:T(8,128)(2,1)} %constant.18.clone.table.forward) | copy-start | bytes 49156
  16.6 18.0 %copy-start.6 = (bf16[128,128]{1,0:T(8,128)(2,1)S(1)}, bf16[128,128]{1,0:T(8,128)(2,1)}, u32[]{:S(2)}) copy-start(bf16[128,128]{1,0:T(8,128)(2,1)} %constant.19.clone.inverse.table) | copy-start | bytes 98308
  17.5 44.4 %copy-start.4 = (bf16[512,256]{1,0:T(8,128)(2,1)S(1)}, bf16[512,256]{1,0:T(8,128)(2,1)}, u32[]{:S(2)}) copy-start(bf16[512,256]{1,0:T(8,128)(2,1)} %constant.25.clone.next_table) | copy-start | bytes 786436
  17.8 58.3 %copy-start.9 = (bf16[64,64]{1,0:T(8,128)(2,1)S(1)}, bf16[64,64]{1,0:T(8,128)(2,1)}, u32[]{:S(2)}) copy-start(bf16[64,64]{1,0:T(8,128)(2,1)} %constant.20.clone.table.forward) | copy-start | bytes 24580
  19.6 1.0 copy-start.1
  20.5 63.5 %copy-start.8 = (bf16[64,128]{1,0:T(8,128)(2,1)S(1)}, bf16[64,128]{1,0:T(8,128)(2,1)}, u32[]{:S(2)}) copy-start(bf16[64,128]{1,0:T(8,128)(2,1)} %constant.21.clone.inverse.table) | copy-start | bytes 49156
  24.1 37.7 %copy-start.2 = (bf16[32,128,128]{2,1,0:T(8,128)(2,1)S(1)}, bf16[32,128,128]{2,1,0:T(8,128)(2,1)}, u32[]{:S(2)}) copy-start(bf16[32,128,128]{2,1,0:T(8,128)(2,1)} %copy-done.1) | copy-start | bytes 3145732
  24.1 37.7 %copy-start.5 = (bf16[256,512]{1,0:T(8,128)(2,1)S(1)}, bf16[256,512]{1,0:T(8,128)(2,1)}, u32[]{:S(2)}) copy-start(bf16[256,512]{1,0:T(8,128)(2,1)} %constant.24.clone.table) | copy-start | bytes 786436
  24.5 81.6 %copy-start.3 = (bf16[256,512]{1,0:T(8,128)(2,1)S(1)}, bf16[256,512]{1,0:T(8,128)(2,1)}, u32[]{:S(2)}) copy-start(bf16[256,512]{1,0:T(8,128)(2,1)} %constant.26.clone.table) | copy-start | bytes 786436
  24.5 81.6 %copy-start.13 = (f32[32]{0:T(128)S(1)}, f32[32]{0:T(128)}, u32[]{:S(2)}) copy-start(f32[32]{0:T(128)} %bias.3) | copy-start | bytes 388

commit v6 on v5

--- a/solution.py
+++ b/solution.py
@@ -193,7 +193,7 @@
                 sums[2 * k + 1] = sums[2 * k + 1] + (w_real * imag + w_imag * real)
         return tuple(sums)
 
-    sums = lax.fori_loop(0, 8, step, tuple(jnp.zeros((C, 128), F32) for _ in range(4)))
+    sums = lax.fori_loop(0, 8, step, tuple(jnp.zeros((C, 128), F32) for _ in range(4)), unroll=4)
     for k in range(2):
         for r in range(2):
             for h in range(4):
@@ -262,11 +262,10 @@
     collect_groups(received, spread, 128)
     even = (lanes_of((64, 128)) & 1) == 0
     for g in range(8):
+        out = dot(spread[g], table[...])
         for h in range(4):
-            if h % 2 == 0:
-                out = dot(spread[g], table[:, 128 * h : 128 * h + 256])
             o = 8 * h + g
-            value = gelu(out[:, 128 * (h % 2) : 128 * (h % 2) + 128] + total[o].astype(F32)).astype(BF16)
+            value = gelu(out[:, 128 * h : 128 * h + 128] + total[o].astype(F32)).astype(BF16)
             upper[o] = value
             value = value.astype(F32).reshape(8, 2, 8, 128)
             value = (value[:, 0] + value[:, 1]).reshape(64, 128)

time: 109 us -> 109 us (level)
  no operation moved by 1% of the time
where the time goes in v6:
time: 109 us; the launch traced here: 108 us
  blocking collectives  75.5 us (69%)
  Pallas kernels  14.2 us (13%)
  starting transfers between devices  9.13 us (8%)
  matrix products  4.46 us (4%)
  waiting for transfers between devices  3.59 us (3%)
  local copies, waits for them, and re-layouts  1.29 us (1%)
    all_to_all x7, blocking collectives, exchange(): return lax.all_to_all(x, axis, 0, 0, tiled=True)  75.5 us
    pallas_call x10, Pallas kernels, call(): pl.pallas_call(kernel, out_shape=shapes if len(shapes) > 1 else shapes[0]...  14.2 us
    all_to_all x1, starting transfers between devices, exchange(): return lax.all_to_all(x, axis, 0, 0, tiled=True)  9.13 us
    dot_general x2, matrix products, lay_out(): jnp.einsum('riojmk,mjl->rikol', spectral, place, preferred_element_type=B...  4.46 us
    all_to_all x1, waiting for transfers between devices, exchange(): return lax.all_to_all(x, axis, 0, 0, tiled=True)  3.59 us
  transfers between devices with their start and end apart: 1, of which 1 were waited for; matrix products, arithmetic and copies ran while one was open for 4% of the time, Pallas kernels for 2%

profile of v6, /device:TPU:1, one launch (start us, length us, event | category | flops | bytes accessed | tf_op | source)
XLA Modules:
  0.0 108.4 jit_solution(9401467716150841695)
XLA Ops:
  0.0 3.8 %shard_map.163 = bf16[16,128,128]{2,1,0:T(8,128)(2,1)} custom-call(bf16[4,8,128,128]{3,2,1,0:T(8,128)(2,1)} %bitcast.24, bf16[512,256]{1,0:T(8,128)(2,1)} %constant.22.clone.table_ref), custom_call_target="tpu_custom_call" | custom-call | tf_op jit(solution)/shard_map/pallas_call | solution.py:314
  3.8 9.1 %all-to-all-start = ((bf16[16,128,128]{2,1,0:T(8,128)(2,1)}), bf16[16,128,128]{2,1,0:T(8,128)(2,1)S(1)}, u32[]{:S(2)}, u32[]{:S(2)}) async-start(bf16[16,128,128]{2,1,0:T(8,128)(2,1)} %shard_map.163), calls=%async_computation | async-start | bytes 1048576 | tf_op jit(solution)/shard_map/all_to_all | solution.py:328
  12.9 3.6 %fusion.4 = bf16[2,32,2,32,128]{4,3,2,1,0:T(8,128)(2,1)S(1)} fusion(bf16[4,32,128,1,1,1]{2,1,0,5,4,3:T(8,128)(2,1)} %constant.30, bf16[2,32,32,32,4,2]{3,5,4,2,1,0:T(2,128)(2,1)} %param.18), kind=kOutput, calls=%fused_computation.4 | convolution fusion | flops 134217728 | bytes 2129920 | tf_op jit(solution)/shard_map/riojmk,mjl->rikol/dot_general | solution.py:333
  16.6 0.0 copy-start.6
  16.6 0.9 fusion.7
  17.5 0.2 copy-done
  17.8 1.8 %shard_map.164 = (bf16[32,128,128]{2,1,0:T(8,128)(2,1)S(1)}, bf16[512,512]{1,0:T(8,128)(2,1)S(1)}) custom-call(bf16[32,128,128]{2,1,0:T(8,128)(2,1)S(1)} %bitcast.25, bf16[32,32]{1,0:T(8,128)(2,1)S(1)} %copy-done.10, f32[32]{0:T(128)S(1)} %copy-done.12, bf16[32,32]{1,0:T(8,128)(2,1)S(1)} %copy-done.11), custom_call_target="tpu_custom_call" | custom-call | tf_op jit(solution)/shard_map/pallas_call | solution.py:314
  19.6 1.0 copy-done.1
  20.5 3.6 %all-to-all-done.received = bf16[16,128,128]{2,1,0:T(8,128)(2,1)S(1)} async-done(((bf16[16,128,128]{2,1,0:T(8,128)(2,1)}), bf16[16,128,128]{2,1,0:T(8,128)(2,1)S(1)}, u32[]{:S(2)}, u32[]{:S(2)}) %all-to-all-start) | async-done | bytes 524320 | tf_op jit(solution)/shard_map/all_to_all | solution.py:328
  24.1 0.4 shard_map.165
  24.6 10.0 %all_to_all.40 = bf16[8,64,128]{2,1,0:T(8,128)(2,1)S(1)} all-to-all(bf16[8,64,128]{2,1,0:T(8,128)(2,1)S(1)} %shard_map.165), channel_id=1, replica_groups=mesh['px'=8,'py'=16] {'px'}, dimensions={0} | all-to-all | bytes 262144 | tf_op jit(solution)/shard_map/all_to_all | solution.py:328
  34.6 1.0 shard_map.166
  35.6 8.0 %all_to_all.41.received = bf16[8,64,128]{2,1,0:T(8,128)(2,1)S(1)} all-to-all(bf16[8,64,128]{2,1,0:T(8,128)(2,1)S(1)} %bitcast.30), channel_id=1, replica_groups=mesh['px'=8,'py'=16] {'px'}, dimensions={0} | all-to-all | bytes 262144 | tf_op jit(solution)/shard_map/all_to_all | solution.py:328
  43.6 0.4 shard_map.167
  44.0 17.8 %all_to_all.42.received = bf16[16,128,128]{2,1,0:T(8,128)(2,1)S(1)} all-to-all(bf16[16,128,128]{2,1,0:T(8,128)(2,1)S(1)} %shard_map.167), channel_id=1, replica_groups=mesh['px'=8,'py'=16] {'py'}, dimensions={0} | all-to-all | bytes 1048576 | tf_op jit(solution)/shard_map/all_to_all | solution.py:328
  61.8 2.9 %shard_map.168 = (bf16[32,128,128]{2,1,0:T(8,128)(2,1)S(1)}, bf16[32,32,128]{2,1,0:T(8,128)(2,1)S(1)}, bf16[16,32,128]{2,1,0:T(8,128)(2,1)S(1)}) custom-call(bf16[16,128,128]{2,1,0:T(8,128)(2,1)S(1)} %all_to_all.42.received, bf16[256,512]{1,0:T(8,128)(2,1)S(1)} %copy-done.5, bf16[32,128,128]{2,1,0:T(8,128)(2,1)S(1)} %copy-done.2, bf16[512,256]{1,0:T(8,128)(2,1)S(1)} %copy-done.4), custom_call_target="tpu_custom_call" | custom-call | tf_op jit(solution)/shard_map/pallas_call | solution.py:314
  64.7 11.3 %all_to_all.43.received = bf16[16,32,128]{2,1,0:T(8,128)(2,1)S(1)} all-to-all(bf16[16,32,128]{2,1,0:T(8,128)(2,1)S(1)} %get-tuple-element.28), channel_id=1, replica_groups=mesh['px'=8,'py'=16] {'py'}, dimensions={0} | all-to-all | bytes 262144 | tf_op jit(solution)/shard_map/all_to_all | solution.py:328
  76.1 0.3 shard_map.169
  76.4 7.6 %all_to_all.44 = bf16[8,32,128]{2,1,0:T(8,128)(2,1)S(1)} all-to-all(bf16[8,32,128]{2,1,0:T(8,128)(2,1)S(1)} %shard_map.169), channel_id=1, replica_groups=mesh['px'=8,'py'=16] {'px'}, dimensions={0} | all-to-all | bytes 131072 | tf_op jit(solution)/shard_map/all_to_all | solution.py:328
  84.0 1.0 shard_map.170
  85.0 7.6 %all_to_all.45.received = bf16[8,32,128]{2,1,0:T(8,128)(2,1)S(1)} all-to-all(bf16[8,32,128]{2,1,0:T(8,128)(2,1)S(1)} %bitcast.32), channel_id=1, replica_groups=mesh['px'=8,'py'=16] {'px'}, dimensions={0} | all-to-all | bytes 131072 | tf_op jit(solution)/shard_map/all_to_all | solution.py:328
  92.5 0.3 shard_map.171
  92.9 13.2 %all_to_all.46.received = bf16[16,32,128]{2,1,0:T(8,128)(2,1)S(1)} all-to-all(bf16[16,32,128]{2,1,0:T(8,128)(2,1)S(1)} %shard_map.171), channel_id=1, replica_groups=mesh['px'=8,'py'=16] {'py'}, dimensions={0} | all-to-all | bytes 262144 | tf_op jit(solution)/shard_map/all_to_all | solution.py:328
  106.1 2.3 %shard_map.172 = bf16[4,8,128,128]{3,2,1,0:T(8,128)(2,1)} custom-call(bf16[16,32,128]{2,1,0:T(8,128)(2,1)S(1)} %all_to_all.46.received, bf16[256,512]{1,0:T(8,128)(2,1)S(1)} %copy-done.3, bf16[32,32,128]{2,1,0:T(8,128)(2,1)S(1)} %get-tuple-element.30.pooled, bf16[512,512]{1,0:T(8,128)(2,1)S(1)} %get-tuple-element.31.channels, f32[32]{0:T(128)S(1)} %copy-done.13, ...), custom_call_target="tpu_custom_call" | custom-call | tf_op jit(solution)/shard_map/pallas_call | solution.py:314
  (29 shorter events, 0.1 us)
Async XLA Ops:
  0.0 16.5 %copy-start.15 = (bf16[4,32,128,1,1,1]{2,1,0,5,4,3:T(8,128)(2,1)S(1)}, bf16[4,32,128,1,1,1]{2,1,0,5,4,3:T(8,128)(2,1)}, u32[]{:S(2)}) copy-start(bf16[4,32,128,1,1,1]{2,1,0,5,4,3:T(8,128)(2,1)} %constant.30) | copy-start | bytes 98308
  3.8 20.3 %all-to-all-start = ((bf16[16,128,128]{2,1,0:T(8,128)(2,1)}), bf16[16,128,128]{2,1,0:T(8,128)(2,1)S(1)}, u32[]{:S(2)}, u32[]{:S(2)}) async-start(bf16[16,128,128]{2,1,0:T(8,128)(2,1)} %shard_map.163), calls=%async_computation | async-start | bytes 1048576 | tf_op jit(solution)/shard_map/all_to_all | solution.py:328
  12.9 3.6 %copy-start.14 = (bf16[2,32,32,32,4,2]{3,5,4,2,1,0:T(2,128)(2,1)S(1)}, bf16[2,32,32,32,4,2]{3,5,4,2,1,0:T(2,128)(2,1)}, u32[]{:S(2)}) copy-start(bf16[2,32,32,32,4,2]{3,5,4,2,1,0:T(2,128)(2,1)} %param.21) | copy-start | bytes 3145732
  16.5 1.2 %copy-start = (bf16[32,16,8,128]{3,2,1,0:T(8,128)(2,1)S(1)}, bf16[32,16,8,128]{3,2,1,0:T(8,128)(2,1)}, u32[]{:S(2)}) copy-start(bf16[32,16,8,128]{3,2,1,0:T(8,128)(2,1)} %param.17) | copy-start | bytes 3145732
  16.6 1.2 %copy-start.10 = (bf16[32,32]{1,0:T(8,128)(2,1)S(1)}, bf16[32,32]{1,0:T(8,128)(2,1)}, u32[]{:S(2)}) copy-start(bf16[32,32]{1,0:T(8,128)(2,1)} %mix_fine.1) | copy-start | bytes 6148
  16.6 1.2 %copy-start.11 = (bf16[32,32]{1,0:T(8,128)(2,1)S(1)}, bf16[32,32]{1,0:T(8,128)(2,1)}, u32[]{:S(2)}) copy-start(bf16[32,32]{1,0:T(8,128)(2,1)} %mix_coarse.1) | copy-start | bytes 6148
  16.6 1.2 %copy-start.12 = (f32[32]{0:T(128)S(1)}, f32[32]{0:T(128)}, u32[]{:S(2)}) copy-start(f32[32]{0:T(128)} %bias.2) | copy-start | bytes 388
  16.6 7.6 %copy-start.7 = (bf16[64,128]{1,0:T(8,128)(2,1)S(1)}, bf16[64,128]{1,0:T(8,128)(2,1)}, u32[]{:S(2)}) copy-start(bf16[64,128]{1,0:T(8,128)(2,1)} %constant.18.clone.table.forward) | copy-start | bytes 49156
  16.6 18.0 %copy-start.6 = (bf16[128,128]{1,0:T(8,128)(2,1)S(1)}, bf16[128,128]{1,0:T(8,128)(2,1)}, u32[]{:S(2)}) copy-start(bf16[128,128]{1,0:T(8,128)(2,1)} %constant.19.clone.inverse.table) | copy-start | bytes 98308
  17.5 44.3 %copy-start.4 = (bf16[512,256]{1,0:T(8,128)(2,1)S(1)}, bf16[512,256]{1,0:T(8,128)(2,1)}, u32[]{:S(2)}) copy-start(bf16[512,256]{1,0:T(8,128)(2,1)} %constant.25.clone.next_table) | copy-start | bytes 786436
  17.8 58.3 %copy-start.9 = (bf16[64,64]{1,0:T(8,128)(2,1)S(1)}, bf16[64,64]{1,0:T(8,128)(2,1)}, u32[]{:S(2)}) copy-start(bf16[64,64]{1,0:T(8,128)(2,1)} %constant.20.clone.table.forward) | copy-start | bytes 24580
  19.6 1.0 copy-start.1
  20.5 63.4 %copy-start.8 = (bf16[64,128]{1,0:T(8,128)(2,1)S(1)}, bf16[64,128]{1,0:T(8,128)(2,1)}, u32[]{:S(2)}) copy-start(bf16[64,128]{1,0:T(8,128)(2,1)} %constant.21.clone.inverse.table) | copy-start | bytes 49156
  24.1 37.7 %copy-start.2 = (bf16[32,128,128]{2,1,0:T(8,128)(2,1)S(1)}, bf16[32,128,128]{2,1,0:T(8,128)(2,1)}, u32[]{:S(2)}) copy-start(bf16[32,128,128]{2,1,0:T(8,128)(2,1)} %copy-done.1) | copy-start | bytes 3145732
  24.1 37.7 %copy-start.5 = (bf16[256,512]{1,0:T(8,128)(2,1)S(1)}, bf16[256,512]{1,0:T(8,128)(2,1)}, u32[]{:S(2)}) copy-start(bf16[256,512]{1,0:T(8,128)(2,1)} %constant.24.clone.table) | copy-start | bytes 786436
  24.5 81.5 %copy-start.3 = (bf16[256,512]{1,0:T(8,128)(2,1)S(1)}, bf16[256,512]{1,0:T(8,128)(2,1)}, u32[]{:S(2)}) copy-start(bf16[256,512]{1,0:T(8,128)(2,1)} %constant.26.clone.table) | copy-start | bytes 786436
  24.5 81.5 %copy-start.13 = (f32[32]{0:T(128)S(1)}, f32[32]{0:T(128)}, u32[]{:S(2)}) copy-start(f32[32]{0:T(128)} %bias.3) | copy-start | bytes 388
